TPU v7x, 32 devices: a whole 2x2x4 slice. The times are simulated.
32 devices in a mesh: gx: 4 (over y, core), gy: 2 (over x), gz: 4 (over z).
Axes of the slice: x: 2, y: 2, z: 4, core: 2. Of those that a mesh axis runs over, the one named last changes fastest.
Arguments:
- offsets: float32 [3, 110592], P(None, ('gx', 'gy', 'gz')), may hold values from 0 to 1
- velocities: float32 [3, 110592], P(None, ('gx', 'gy', 'gz')), may hold values from -6 to 6
- masses: float32 [110592], P(('gx', 'gy', 'gz')), may hold values from 0.5 to 2
- active: int32 [110592], P(('gx', 'gy', 'gz')), may hold values from 0 to 1, as said below
- near_local: int32 [864, 2], P(('gx', 'gy', 'gz')), may hold values from 0 to 26
- near_remote: int32 [864, 3, 1], P(('gx', 'gy', 'gz')), may hold values from 0 to 8
- far_list: int32 [864, 5, 2], P(('gx', 'gy', 'gz')), may hold values from 0 to 26
Outputs:
- positions_out: float32 [3, 110592], P(None, ('gx', 'gy', 'gz'))
- velocities_out: float32 [3, 110592], P(None, ('gx', 'gy', 'gz'))
- accel_out: float32 [3, 110592], P(None, ('gx', 'gy', 'gz'))
- time_steps: float32 [2], replicated
Inputs may be any that keep to these rules, and one draw needn't show every extreme that they name: `active`: 0 or 1; each device has its own rate of ones, from 1/64 to 1/4.
All inputs are finite; a program needn't handle non-finite values.
Results may differ from a plain program's by a relative error of at most 0.0003.
Values sent between devices are 32-bit elements; how exact they have to be, the bound alone decides.
No kernel may reach another device: no remote copies, remote signals or barrier semaphores. Data moves between devices by JAX's collectives and lax.ppermute only.
A program may use at most 64 MiB of HBM per device.

v0:
```python
import jax
import jax.numpy as jnp
from jax import lax
from jax.sharding import PartitionSpec as P

TG = 3
SUBSTEPS = 2


GRAV = 0.02
SOFT2 = 0.0025
ETA = 0.15


def partner(block, axis, bit):
    count = lax.axis_size(axis)
    route = []
    for low in range(count):
        high = low | 1 << bit
        if high != low and high < count:
            route += [(low, high), (high, low)]
    return lax.ppermute(block, axis, route)


def tile_corners(tile_grid):
    tile_ids = jnp.arange(tile_grid**3, dtype=jnp.int32)
    return jnp.stack(
        [
            tile_ids // (tile_grid * tile_grid),
            tile_ids // tile_grid % tile_grid,
            tile_ids % tile_grid,
        ]
    ).astype(jnp.float32)


def tile_moments(bodies):
    tile_mass = bodies[3]
    total_mass = jnp.sum(tile_mass, axis=-1)
    center = jnp.sum(bodies[:3] * tile_mass, axis=-1) / total_mass
    relative = bodies[:3] - center[:, :, None]
    square = jnp.sum(relative * relative, axis=0)

    def quad(first_axis, second_axis):
        quad_term = 3.0 * relative[first_axis] * relative[second_axis]
        if first_axis == second_axis:
            quad_term = quad_term - square
        return jnp.sum(tile_mass * quad_term, axis=-1)

    return jnp.stack(
        [
            total_mass,
            center[0],
            center[1],
            center[2],
            quad(0, 0),
            quad(1, 1),
            quad(2, 2),
            quad(0, 1),
            quad(0, 2),
            quad(1, 2),
        ]
    )


def face_index(cut_axis, face_coord, tile_grid):
    strides = (tile_grid * tile_grid, tile_grid, 1)
    others = [axis_id for axis_id in range(3) if axis_id != cut_axis]
    slot_ids = jnp.arange(tile_grid * tile_grid, dtype=jnp.int32)
    return (
        face_coord * strides[cut_axis]
        + slot_ids // tile_grid * strides[others[0]]
        + slot_ids % tile_grid * strides[others[1]]
    )


def level_place(level, z_bits, y_bits):
    if level < z_bits:
        return (2, level, 0 if level == 0 else -1)
    if level < z_bits + y_bits:
        return (1, level - z_bits, 1 if level == z_bits else -1)
    return (0, level - z_bits - y_bits, 2 if level == z_bits + y_bits else -1)


def signed_shift(own_bit, span):
    return jnp.where(own_bit == 0, span, -span).astype(jnp.float32)


def far_field(target, moments):
    relative = target[:, :, None] - moments[1:4, None, :]
    distance = jnp.sum(relative * relative, axis=0) + SOFT2
    inverse = lax.rsqrt(distance)
    inverse_sq = inverse * inverse
    cube = inverse * inverse_sq
    fifth = cube * inverse_sq
    seventh = fifth * inverse_sq
    quad_dot = jnp.stack(
        [
            moments[4] * relative[0] + moments[7] * relative[1] + moments[8] * relative[2],
            moments[7] * relative[0] + moments[5] * relative[1] + moments[9] * relative[2],
            moments[8] * relative[0] + moments[9] * relative[1] + moments[6] * relative[2],
        ]
    )
    quad_form = jnp.sum(relative * quad_dot, axis=0)
    field = -moments[0] * relative * cube + quad_dot * fifth - 2.5 * quad_form * relative * seventh
    return jnp.sum(field, axis=2)


def tile_force(target, sources, moments):
    relative = sources[:3, None, :] - target[:, :, None]
    distance = jnp.sum(relative * relative, axis=0) + SOFT2
    inverse = lax.rsqrt(distance)
    strength = sources[3][None, :] * inverse * inverse * inverse
    near_sum = jnp.sum(relative * strength[None], axis=2)
    return GRAV * (near_sum + far_field(target, moments))


def force_item(packed_item):
    return tile_force(packed_item[0], packed_item[1], packed_item[2])


def accelerate(bodies, face_stack, moment_stack, near_local, near_remote, far_list):
    count_tiles = bodies.shape[1]
    tile_size = bodies.shape[2]
    near_slots = face_stack.shape[1]
    slots = face_stack.shape[2]
    moment_levels = moment_stack.shape[1]
    local_src = jnp.take(bodies, near_local, axis=1)
    flat_faces = face_stack.reshape(4, near_slots * slots, tile_size)
    remote_index = (
        near_remote + (jnp.arange(near_slots, dtype=jnp.int32) * slots)[None, :, None]
    ).reshape(count_tiles, -1)
    remote = jnp.take(flat_faces, remote_index, axis=1)
    sources = (
        jnp.concatenate([local_src, remote], axis=2).reshape(4, count_tiles, -1).transpose(1, 0, 2)
    )
    far_index = (
        far_list + (jnp.arange(moment_levels, dtype=jnp.int32) * count_tiles)[None, :, None]
    ).reshape(count_tiles, -1)
    picked = jnp.take(
        moment_stack.reshape(10, moment_levels * count_tiles), far_index, axis=1
    ).transpose(1, 0, 2)
    targets = bodies[:3].transpose(1, 0, 2)
    result = lax.map(force_item, (targets, sources, picked))
    return result.transpose(1, 0, 2)


def body(offsets, velocities, masses, active, near_local, near_remote, far_list):
    tile_grid = TG
    count_tiles = near_local.shape[0]
    tile_size = masses.shape[0] // count_tiles
    levels = far_list.shape[1]
    position = offsets.reshape(3, count_tiles, tile_size) + tile_corners(tile_grid)[:, :, None]
    velocity = velocities.reshape(3, count_tiles, tile_size)
    tile_mass = masses.reshape(count_tiles, tile_size)
    weight = active.reshape(count_tiles, tile_size).astype(jnp.float32)
    device_index = lax.axis_index(("gx", "gy", "gz"))
    z_bits = lax.axis_size("gz").bit_length() - 1
    y_bits = lax.axis_size("gy").bit_length() - 1
    sequence = list(range(levels))
    steps_taken = []
    acceleration = jnp.zeros_like(position)
    for substep in range(SUBSTEPS):
        bodies = jnp.concatenate([position, tile_mass[None]], axis=0)
        face_list = [None, None, None]
        moment_list = [None] * levels
        for level in sequence:
            own_bit = jnp.right_shift(device_index, level) & 1
            cut_axis, place, near_slot = level_place(level, z_bits, y_bits)
            shift = signed_shift(own_bit, tile_grid * 2**place)
            face_tiles = None
            partner_bodies = partner(bodies, ("gx", "gy", "gz"), level)
            moments = tile_moments(partner_bodies)
            if near_slot >= 0:
                face_coord = jnp.where(own_bit == 1, tile_grid - 1, 0).astype(jnp.int32)
                face_tiles = jnp.take(
                    partner_bodies, face_index(cut_axis, face_coord, tile_grid), axis=1
                )
            moment_list[level] = moments.at[1 + cut_axis].add(shift)
            if near_slot >= 0:
                face_list[near_slot] = face_tiles.at[cut_axis].add(shift)
        acceleration = accelerate(
            bodies,
            jnp.stack(face_list, axis=1),
            jnp.stack(moment_list, axis=1),
            near_local,
            near_remote,
            far_list,
        )
        magnitude = jnp.sqrt(jnp.sum(acceleration * acceleration, axis=0))
        local_largest = jnp.max(jnp.where(weight > 0, magnitude, 0.0))
        largest = lax.pmax(local_largest, ("gx", "gy", "gz"))
        time_step = ETA / jnp.sqrt(largest + 1e-06)
        velocity = velocity + weight[None] * acceleration * time_step
        position = position + weight[None] * velocity * time_step
        steps_taken.append(time_step)
    return (
        position.reshape(3, -1),
        velocity.reshape(3, -1),
        (weight[None] * acceleration).reshape(3, -1),
        jnp.stack(steps_taken),
    )


def solution(mesh):
    return jax.shard_map(
        body,
        mesh=mesh,
        in_specs=(
            P(None, ("gx", "gy", "gz")),
            P(None, ("gx", "gy", "gz")),
            P(("gx", "gy", "gz")),
            P(("gx", "gy", "gz")),
            P(("gx", "gy", "gz"), None),
            P(("gx", "gy", "gz"), None, None),
            P(("gx", "gy", "gz"), None, None),
        ),
        out_specs=(
            P(None, ("gx", "gy", "gz")),
            P(None, ("gx", "gy", "gz")),
            P(None, ("gx", "gy", "gz")),
            P(),
        ),
        check_vma=False,
    )
```

profile of v0, /device:TPU:0, one launch (start us, length us, event | category | flops | bytes accessed | tf_op | source)
XLA Modules:
  0.0 187.4 jit_solution(545022564436974631)
XLA Ops:
  0.7 0.8 reshape.969
  1.7 0.7 copy-done.1
  2.4 3.1 %collective-permute-start.4 = (f32[4,27,128]{2,0,1:T(4,128)S(1)}, f32[4,27,128]{2,0,1:T(4,128)S(1)}, u32[]{:S(2)}, u32[]{:S(2)}) collective-permute-start(f32[4,27,128]{2,0,1:T(4,128)S(1)} %pad_maximum_fusion.3), channel_id=1, source_target_pairs={{0,16},{16,0},{1,17},{17,1},{2,18},{18,2},{3,19},{19,3},{4,20},{20... | collective-permute-start | bytes 165896 | tf_op jit(solution)/shard_map/ppermute | solution.py:22
  5.5 1.6 collective-permute-start.1
  7.1 2.6 %collective-permute-start.3 = (f32[4,27,128]{2,1,0:T(8,128)S(1)}, f32[4,27,128]{2,1,0:T(8,128)S(1)}, u32[]{:S(2)}, u32[]{:S(2)}) collective-permute-start(f32[4,27,128]{2,1,0:T(8,128)S(1)} %copy.498), channel_id=1, source_target_pairs={{0,2},{2,0},{1,3},{3,1},{4,6},{6,4},{5,7},{7,5},{8,10},{10,8},{9,1... | collective-permute-start | bytes 165896 | tf_op jit(solution)/shard_map/ppermute | solution.py:22
  9.7 1.6 collective-permute-start
  11.6 0.6 copy-done.4
  12.3 0.7 copy-done.5
  13.7 0.6 gather_fusion
  19.0 1.0 gather_fusion.5
  20.4 0.6 gather_fusion.1
  21.1 0.6 gather_fusion.2
  21.8 0.6 gather_fusion.3
  22.7 0.7 gather_fusion.4
  23.6 32.3 %while.36 = (s32[]{:T(128)}, f32[27,3,128]{2,1,0:T(4,128)S(1)}, f32[27,4,640]{2,1,0:T(4,128)S(1)}, f32[27,3,128]{2,0,1:T(8,128)S(1)}, f32[27,10,10]{2,0,1:T(8,12...) while((s32[]{:T(128)}, f32[27,3,128]{2,1,0:T(4,128)S(1)}, ...), condition=%wide.region_51.56_spmd, body=%wide.region_45.0_spmd.sunk | while | flops 1817620 | bytes 1512617 | solution.py:143
  56.0 0.6 fusion.192
  56.6 38.3 %pmax.14 = f32[]{:T(128)} all-reduce(f32[]{:T(128)} %get-tuple-element.444), channel_id=1, replica_groups=mesh['gx'=4,'gy'=2,'gz'=4] {'gx','gy','gz'}, use_global_device_ids=true, to_apply=%region_54.59 | all-reduce | flops 1 | bytes 8 | tf_op jit(solution)/shard_map/pmax | solution.py:191
  95.7 2.5 %collective-permute-start.9 = (f32[4,27,128]{2,1,0:T(8,128)S(1)}, f32[4,27,128]{2,1,0:T(8,128)S(1)}, u32[]{:S(2)}, u32[]{:S(2)}) collective-permute-start(f32[4,27,128]{2,1,0:T(8,128)S(1)} %pad_maximum_fusion.2), channel_id=1, source_target_pairs={{0,16},{16,0},{1,17},{17,1},{2,18},{18,2},{3,19},{19,3},{4,20},{20... | collective-permute-start | bytes 165896 | tf_op jit(solution)/shard_map/ppermute | solution.py:22
  98.8 1.7 collective-permute-start.8
  101.0 0.6 gather_fusion.6
  103.0 2.0 %collective-permute-done.8 = f32[4,27,128]{2,1,0:T(8,128)S(1)} collective-permute-done((f32[4,27,128]{2,1,0:T(8,128)S(1)}, f32[4,27,128]{2,1,0:T(8,128)S(1)}, u32[]{:S(2)}, u32[]{:S(2)}) %collective-permute-start.8) | collective-permute-done | bytes 55328 | tf_op jit(solution)/shard_map/ppermute | solution.py:22
  107.6 1.0 gather_fusion.11
  109.0 0.6 gather_fusion.7
  109.7 0.6 gather_fusion.8
  111.3 0.7 gather_fusion.10
  112.2 32.3 %while.37 = (s32[]{:T(128)}, f32[27,3,128]{2,1,0:T(4,128)S(1)}, f32[27,4,640]{2,1,0:T(4,128)S(1)}, f32[27,3,128]{2,0,1:T(8,128)S(1)}, f32[27,10,10]{2,0,1:T(8,12...) while((s32[]{:T(128)}, f32[27,3,128]{2,1,0:T(4,128)S(1)}, ...), condition=%wide.region_106.111_spmd, body=%wide.region_100.110_spmd.sunk | while | flops 1817620 | bytes 1512617 | solution.py:143
  144.6 0.6 fusion.191
  145.2 39.0 %pmax.15 = f32[]{:T(128)} all-reduce(f32[]{:T(128)} %fusion.191), channel_id=1, replica_groups=mesh['gx'=4,'gy'=2,'gz'=4] {'gx','gy','gz'}, use_global_device_ids=true, to_apply=%region_109.114 | all-reduce | flops 1 | bytes 8 | tf_op jit(solution)/shard_map/pmax | solution.py:191
  184.9 0.7 copy.637
  185.5 0.7 copy.638
  186.2 0.7 copy.636
  186.8 0.6 pad_maximum_fusion.6
  (1183 shorter events, 72.6 us)
Async XLA Ops:
  1.6 0.7 copy-start.1
  2.4 12.9 %collective-permute-start.4 = (f32[4,27,128]{2,0,1:T(4,128)S(1)}, f32[4,27,128]{2,0,1:T(4,128)S(1)}, u32[]{:S(2)}, u32[]{:S(2)}) collective-permute-start(f32[4,27,128]{2,0,1:T(4,128)S(1)} %pad_maximum_fusion.3), channel_id=1, source_target_pairs={{0,16},{16,0},{1,17},{17,1},{2,18},{18,2},{3,19},{19,3},{4,20},{20... | collective-permute-start | bytes 165896 | tf_op jit(solution)/shard_map/ppermute | solution.py:22
  5.5 5.8 %copy-start.3 = (s32[27,5,2]{0,2,1:T(2,128)S(1)}, s32[27,5,2]{0,2,1:T(2,128)}, u32[]{:S(2)}) copy-start(s32[27,5,2]{0,2,1:T(2,128)} %param.57) | copy-start | bytes 3244
  5.5 10.6 %collective-permute-start.2 = (f32[4,27,128]{2,1,0:T(8,128)S(1)}, f32[4,27,128]{2,1,0:T(8,128)S(1)}, u32[]{:S(2)}, u32[]{:S(2)}) collective-permute-start(f32[4,27,128]{2,1,0:T(8,128)S(1)} %copy.498), channel_id=1, source_target_pairs={{0,8},{8,0},{1,9},{9,1},{2,10},{10,2},{3,11},{11,3},{4,12},{12,4},... | collective-permute-start | bytes 165896 | tf_op jit(solution)/shard_map/ppermute | solution.py:22
  5.5 10.8 %collective-permute-start.1 = (f32[4,27,128]{2,1,0:T(8,128)S(1)}, f32[4,27,128]{2,1,0:T(8,128)S(1)}, u32[]{:S(2)}, u32[]{:S(2)}) collective-permute-start(f32[4,27,128]{2,1,0:T(8,128)S(1)} %copy.498), channel_id=1, source_target_pairs={{0,4},{4,0},{1,5},{5,1},{2,6},{6,2},{3,7},{7,3},{8,12},{12,8},{9,1... | collective-permute-start | bytes 165896 | tf_op jit(solution)/shard_map/ppermute | solution.py:22
  7.1 11.1 %collective-permute-start.3 = (f32[4,27,128]{2,1,0:T(8,128)S(1)}, f32[4,27,128]{2,1,0:T(8,128)S(1)}, u32[]{:S(2)}, u32[]{:S(2)}) collective-permute-start(f32[4,27,128]{2,1,0:T(8,128)S(1)} %copy.498), channel_id=1, source_target_pairs={{0,2},{2,0},{1,3},{3,1},{4,6},{6,4},{5,7},{7,5},{8,10},{10,8},{9,1... | collective-permute-start | bytes 165896 | tf_op jit(solution)/shard_map/ppermute | solution.py:22
  9.7 6.9 %collective-permute-start = (f32[4,27,128]{2,1,0:T(8,128)S(1)}, f32[4,27,128]{2,1,0:T(8,128)S(1)}, u32[]{:S(2)}, u32[]{:S(2)}) collective-permute-start(f32[4,27,128]{2,1,0:T(8,128)S(1)} %copy.498), channel_id=1, source_target_pairs={{0,1},{1,0},{2,3},{3,2},{4,5},{5,4},{6,7},{7,6},{8,9},{9,8},{10,11... | collective-permute-start | bytes 165896 | tf_op jit(solution)/shard_map/ppermute | solution.py:22
  11.5 0.7 copy-start.4
  12.3 0.7 copy-start.5
  13.7 0.8 copy-start
  14.5 0.8 copy-start.2
  95.7 6.1 %collective-permute-start.9 = (f32[4,27,128]{2,1,0:T(8,128)S(1)}, f32[4,27,128]{2,1,0:T(8,128)S(1)}, u32[]{:S(2)}, u32[]{:S(2)}) collective-permute-start(f32[4,27,128]{2,1,0:T(8,128)S(1)} %pad_maximum_fusion.2), channel_id=1, source_target_pairs={{0,16},{16,0},{1,17},{17,1},{2,18},{18,2},{3,19},{19,3},{4,20},{20... | collective-permute-start | bytes 165896 | tf_op jit(solution)/shard_map/ppermute | solution.py:22
  98.2 3.8 %collective-permute-start.7 = (f32[4,27,128]{2,1,0:T(8,128)S(1)}, f32[4,27,128]{2,1,0:T(8,128)S(1)}, u32[]{:S(2)}, u32[]{:S(2)}) collective-permute-start(f32[4,27,128]{2,1,0:T(8,128)S(1)} %pad_maximum_fusion.2), channel_id=1, source_target_pairs={{0,8},{8,0},{1,9},{9,1},{2,10},{10,2},{3,11},{11,3},{4,12},{12,4},... | collective-permute-start | bytes 165896 | tf_op jit(solution)/shard_map/ppermute | solution.py:22
  98.2 4.5 %collective-permute-start.6 = (f32[4,27,128]{2,1,0:T(8,128)S(1)}, f32[4,27,128]{2,1,0:T(8,128)S(1)}, u32[]{:S(2)}, u32[]{:S(2)}) collective-permute-start(f32[4,27,128]{2,1,0:T(8,128)S(1)} %pad_maximum_fusion.2), channel_id=1, source_target_pairs={{0,4},{4,0},{1,5},{5,1},{2,6},{6,2},{3,7},{7,3},{8,12},{12,8},{9,1... | collective-permute-start | bytes 165896 | tf_op jit(solution)/shard_map/ppermute | solution.py:22
  98.8 6.2 %collective-permute-start.8 = (f32[4,27,128]{2,1,0:T(8,128)S(1)}, f32[4,27,128]{2,1,0:T(8,128)S(1)}, u32[]{:S(2)}, u32[]{:S(2)}) collective-permute-start(f32[4,27,128]{2,1,0:T(8,128)S(1)} %pad_maximum_fusion.2), channel_id=1, source_target_pairs={{0,2},{2,0},{1,3},{3,1},{4,6},{6,4},{5,7},{7,5},{8,10},{10,8},{9,1... | collective-permute-start | bytes 165896 | tf_op jit(solution)/shard_map/ppermute | solution.py:22
  100.5 4.9 %collective-permute-start.5 = (f32[4,27,128]{2,1,0:T(8,128)S(1)}, f32[4,27,128]{2,1,0:T(8,128)S(1)}, u32[]{:S(2)}, u32[]{:S(2)}) collective-permute-start(f32[4,27,128]{2,1,0:T(8,128)S(1)} %pad_maximum_fusion.2), channel_id=1, source_target_pairs={{0,1},{1,0},{2,3},{3,2},{4,5},{5,4},{6,7},{7,6},{8,9},{9,8},{10,11... | collective-permute-start | bytes 165896 | tf_op jit(solution)/shard_map/ppermute | solution.py:22
where the time goes:
time: 188 us; the launch traced here: 187 us
  blocking collectives  77.3 us (41%)
  other arithmetic  59 us (31%)
  local copies, waits for them, and re-layouts  26.1 us (14%)
  starting transfers between devices  14.1 us (8%)
  loops' own time  5.31 us (3%)
  between operations  3.01 us (2%)
  waiting for transfers between devices  2.58 us (1%)
    pmax x2, blocking collectives, body(): largest = lax.pmax(local_largest, ('gx', 'gy', 'gz'))  77.3 us
    ppermute x10, starting transfers between devices, partner(): return lax.ppermute(block, axis, route)  14.1 us
    reduce_sum x54, other arithmetic, tile_force(): near_sum = jnp.sum(relative * strength[None], axis=2)  13.9 us
    reduce_sum x54, other arithmetic, tile_force(): distance = jnp.sum(relative * relative, axis=0) + SOFT2  8.47 us
    add x54, other arithmetic, far_field(): moments[4] * relative[0] + moments[7] * relative[1]  7.12 us
    reduce_sum x54, other arithmetic, far_field(): return jnp.sum(field, axis=2)  5.63 us
    reduce_sum x54, other arithmetic, far_field(): quad_form = jnp.sum(relative * quad_dot, axis=0)  5.57 us
    another operation x2, loops' own time, accelerate(): result = lax.map(force_item, (targets, sources, picked))  5.31 us
  transfers between devices with their start and end apart: 10, of which 3 were waited for; matrix products, arithmetic and copies ran while one was open for 3% of the time, Pallas kernels for 0%

commit v1 on v0

v1 whole, which is shorter than its diff:
```python
import functools

import jax
import jax.numpy as jnp
from jax import lax
from jax.experimental import pallas as pl
from jax.experimental.pallas import tpu as pltpu
from jax.sharding import PartitionSpec as P

SUBSTEPS = 2
GRAV = 0.02
SOFT2 = 0.0025
ETA = 0.15
AXES = ("gx", "gy", "gz")
F32 = jnp.float32
BF16 = jnp.bfloat16
FAST_GROUPS = 6
STEP = 16


def up8(count):
    return (count + 7) // 8 * 8


def level_place(level, z_bits, y_bits):
    if level < z_bits:
        return (2, level, 0 if level == 0 else -1)
    if level < z_bits + y_bits:
        return (1, level - z_bits, 1 if level == z_bits else -1)
    return (0, level - z_bits - y_bits, 2 if level == z_bits + y_bits else -1)


class Plan:
    def __init__(self, mesh, count_tiles, tile_size, levels, km, kl, kn):
        self.tiles = count_tiles
        self.size = tile_size
        self.rows = up8(count_tiles)
        self.grid = round(count_tiles ** (1 / 3))
        self.face = self.grid * self.grid
        self.levels = levels
        self.km = km
        self.kl = kl
        self.kn = kn
        self.devices = mesh.size
        z_bits = mesh.shape["gz"].bit_length() - 1
        y_bits = mesh.shape["gy"].bit_length() - 1
        x_bits = mesh.shape["gx"].bit_length() - 1
        self.place = [level_place(level, z_bits, y_bits) for level in range(levels)]
        self.near_level = [None] * 3
        for level, (_, _, slot) in enumerate(self.place):
            if slot >= 0:
                self.near_level[slot] = level
        self.frows = up8(3 * self.face)
        self.row_u = self.frows
        self.row_m = 2 * self.frows
        self.row_t = self.row_m + up8(self.face)
        self.near_rows = self.row_t + self.rows
        self.stages = []
        start = 0
        for bits in (z_bits, y_bits, x_bits):
            low = start
            while low < start + bits:
                top = min(low + 2, start + bits)
                self.stages.append(list(range(low, top)))
                low = top
            start += bits


def lane_sum(values):
    return jnp.sum(values, axis=1, keepdims=True)


def split3(values):
    high = values.astype(BF16)
    rest = values - high.astype(F32)
    middle = rest.astype(BF16)
    low = (rest - middle.astype(F32)).astype(BF16)
    return high, middle, low


def dot_nt(left, right):
    return lax.dot_general(left, right, (((1,), (1,)), ((), ())), preferred_element_type=F32)


def dot_nn(left, right):
    return lax.dot_general(left, right, (((1,), (0,)), ((), ())), preferred_element_type=F32)


PAIRS = ((0, 0), (1, 1), (2, 2), (0, 1), (0, 2), (1, 2))


def moment_table(mass, parts):
    shape = mass.shape
    lane = lax.broadcasted_iota(jnp.int32, shape, 1)
    total = lane_sum(mass)
    columns = [(0, total)]
    rel = []
    for k, part in enumerate(parts):
        line = []
        for c in range(3):
            center = lane_sum(mass * part[c]) / total
            columns.append((k * STEP + 1 + c, center))
            line.append(part[c] - center)
        rel.append(line)
    weighted = [[mass * line[c] for c in range(3)] for line in rel]
    count = len(parts)
    for k in range(2 * count - 1):
        second = []
        for a, b in PAIRS:
            term = None
            for i in range(count):
                j = k - i
                if 0 <= j < count:
                    item = weighted[i][a] * rel[j][b]
                    term = item if term is None else term + item
            second.append(lane_sum(term))
        trace = second[0] + second[1] + second[2]
        for q in range(6):
            value = 3.0 * second[q] - trace if q < 3 else 3.0 * second[q]
            columns.append((k * STEP + 4 + q, value))
    table = jnp.zeros(shape, F32)
    for where, value in columns:
        table = jnp.where(lane == where, value, table)
    return table


def device_bits(levels):
    device = lax.axis_index(AXES)
    return [jnp.right_shift(device, level) & 1 for level in range(levels)]


def face_rows(plan, slot, bit):
    cut = 2 - slot
    grid = plan.grid
    strides = (grid * grid, grid, 1)
    others = [axis for axis in range(3) if axis != cut]
    coord = jnp.where(bit == 1, 0, grid - 1)
    base = coord * strides[cut]
    return [
        base + s // grid * strides[others[0]] + s % grid * strides[others[1]]
        for s in range(plan.face)
    ]


def first_kernel(plan, off_ref, vel_ref, mass_ref, act_ref, base_ref, mom_ref, *near_refs):
    tiles, rows, size, grid = plan.tiles, plan.rows, plan.size, plan.grid
    tile = lax.broadcasted_iota(jnp.int32, (rows, size), 0)
    base_ref[...] = jnp.zeros(base_ref.shape, F32)
    for t in range(tiles):
        lanes = pl.ds(t * size, size)
        for c in range(3):
            base_ref[c, pl.ds(t, 1), :] = off_ref[pl.ds(c, 1), lanes]
            base_ref[4 + c, pl.ds(t, 1), :] = vel_ref[pl.ds(c, 1), lanes]
    base_ref[3, pl.ds(0, tiles), :] = mass_ref[...]
    base_ref[7, pl.ds(0, tiles), :] = act_ref[...].astype(F32)
    corners = (tile // (grid * grid), tile // grid % grid, tile % grid)
    inside = tile < tiles
    act = base_ref[7]
    position = []
    for c in range(3):
        value = jnp.where(inside, base_ref[c] + corners[c].astype(F32), 0.0)
        base_ref[c] = value
        position.append(value)
        base_ref[4 + c] = base_ref[4 + c] * act
    mass = jnp.where(inside, base_ref[3], 1.0)
    base_ref[3] = mass
    table = moment_table(mass, [position])
    mom_ref[...] = table
    bits = device_bits(plan.levels)
    for slot, ref in enumerate(near_refs):
        ref[pl.ds(plan.row_t, rows), :] = table
        for s, row in enumerate(face_rows(plan, slot, bits[plan.near_level[slot]])):
            for c in range(3):
                ref[pl.ds(c * plan.face + s, 1), :] = base_ref[c, pl.ds(row, 1), :]
                ref[pl.ds(plan.row_u + c * plan.face + s, 1), :] = base_ref[4 + c, pl.ds(row, 1), :]
            ref[pl.ds(plan.row_m + s, 1), :] = base_ref[3, pl.ds(row, 1), :]


def far_field(plan, far_ref, tables, target):
    rows, size = plan.rows, plan.size
    cell = lax.broadcasted_iota(jnp.int32, (rows, rows), 1)
    total = [jnp.zeros((rows, size), F32) for _ in range(3)]
    for level in range(plan.levels):
        parts = split3(tables[level])
        for k in range(plan.km):
            where = level * plan.km + k
            pick = jnp.where(far_ref[:, pl.ds(where, 1)] == cell, 1.0, 0.0).astype(BF16)
            got = dot_nn(pick, parts[0]) + dot_nn(pick, parts[1]) + dot_nn(pick, parts[2])
            q = [jnp.broadcast_to(got[:, p : p + 1], (rows, size)) for p in range(10)]
            r = [target[c] - q[1 + c] for c in range(3)]
            inverse = lax.rsqrt(r[0] * r[0] + r[1] * r[1] + r[2] * r[2] + SOFT2)
            inverse_sq = inverse * inverse
            cube = inverse * inverse_sq
            fifth = cube * inverse_sq
            dot = [
                q[4] * r[0] + q[7] * r[1] + q[8] * r[2],
                q[7] * r[0] + q[5] * r[1] + q[9] * r[2],
                q[8] * r[0] + q[9] * r[1] + q[6] * r[2],
            ]
            form = r[0] * dot[0] + r[1] * dot[1] + r[2] * dot[2]
            scale = q[0] * cube + 2.5 * form * (fifth * inverse_sq)
            for c in range(3):
                total[c] = total[c] + (dot[c] * fifth - scale * r[c])
    return total


def near_field(plan, list_ref, src_ref, face_ref, rank_ref, row_ref, comp_ref, part_ref):
    tiles, size = plan.tiles, plan.size
    kl, kn = plan.kl, plan.kn
    per_tile = kl + 3 * kn
    fast = FAST_GROUPS * 8
    last = tiles - 1

    def one_hot(t, first, count):
        slot = lax.broadcasted_iota(jnp.int32, (count, size), 0).astype(F32) + first
        return rank_ref[pl.ds(t, 1), :] == slot

    def compact(t, first, count):
        pick = jnp.where(one_hot(t, first, count), 1.0, 0.0).astype(BF16)
        sub = lax.broadcasted_iota(jnp.int32, (8, size), 0)
        own = jnp.where(
            sub == 0,
            src_ref[0, pl.ds(t, 1), :],
            jnp.where(sub == 1, src_ref[1, pl.ds(t, 1), :], src_ref[2, pl.ds(t, 1), :]),
        )
        high, middle, low = split3(own)
        return dot_nt(pick, high) + dot_nt(pick, middle) + dot_nt(pick, low)

    def source_rows(t):
        found = []
        for s in range(per_tile):
            index = list_ref[t * per_tile + s]
            if s < kl:
                found.append([src_ref[c, pl.ds(index, 1), :] for c in range(4)])
            else:
                slot = (s - kl) // kn
                found.append([face_ref[slot, c, pl.ds(index, 1), :] for c in range(4)])
        return found

    def pair_sums(packed, sources):
        here = [jnp.broadcast_to(packed[:, c : c + 1], (8, size)) for c in range(3)]
        sums = None
        for source in sources:
            r = [source[c] - here[c] for c in range(3)]
            inverse = lax.rsqrt(r[0] * r[0] + r[1] * r[1] + r[2] * r[2] + SOFT2)
            strength = source[3] * inverse * (inverse * inverse)
            new = [r[c] * strength for c in range(3)]
            sums = new if sums is None else [sums[c] + new[c] for c in range(3)]
        return sums

    def scatter(t):
        out = [None] * 3
        for g in range(FAST_GROUPS):
            mask = one_hot(t, g * 8, 8)
            for c in range(3):
                column = lane_sum(part_ref[t, g, c])
                value = jnp.where(mask, column, 0.0)
                out[c] = value if out[c] is None else out[c] + value
        for c in range(3):
            row_ref[c, pl.ds(t, 1), :] = jnp.sum(out[c], axis=0, keepdims=True)

    def force(t):
        sources = source_rows(t)
        for g in range(FAST_GROUPS):
            sums = pair_sums(comp_ref[t, pl.ds(g * 8, 8), :], sources)
            for c in range(3):
                part_ref[t, g, c] = sums[c]

    comp_ref[0, :, pl.ds(0, 8)] = compact(0, 0, fast)

    def body(t, carry):
        scatter(jnp.maximum(t - 1, 0))
        force(t)
        after = jnp.minimum(t + 1, last)
        comp_ref[after, :, pl.ds(0, 8)] = compact(after, 0, fast)
        return carry

    lax.fori_loop(0, tiles, body, 0)
    scatter(last)

    @pl.when(list_ref[tiles * per_tile + tiles] > fast)
    def _():
        def tile_rest(t, carry):
            def group(g, inner):
                packed = compact(t, g * 8, 8)
                sums = pair_sums(packed, source_rows(t))
                mask = one_hot(t, g * 8, 8)
                for c in range(3):
                    value = jnp.where(mask, lane_sum(sums[c]), 0.0)
                    old = row_ref[c, pl.ds(t, 1), :]
                    row_ref[c, pl.ds(t, 1), :] = old + jnp.sum(value, axis=0, keepdims=True)
                return inner

            groups = (list_ref[tiles * per_tile + t] + 7) // 8
            lax.fori_loop(FAST_GROUPS, groups, group, 0)
            return carry

        lax.fori_loop(0, tiles, tile_rest, 0)


def shift_of(plan, level, bit):
    _, place, _ = plan.place[level]
    span = float(plan.grid * 2**place)
    return jnp.where(bit == 0, span, -span).astype(F32)


def forces(plan, act, target, tables, list_ref, far_ref, src_ref, face_ref, scratch):
    rank_ref, row_ref, comp_ref, part_ref = scratch
    rows, size = plan.rows, plan.size
    below = lax.broadcasted_iota(jnp.int32, (size, size), 0) < lax.broadcasted_iota(
        jnp.int32, (size, size), 1
    )
    rank = dot_nn(act.astype(BF16), jnp.where(below, 1.0, 0.0).astype(BF16))
    rank_ref[...] = jnp.where(act > 0, rank, -1.0)
    row_ref[...] = jnp.zeros(row_ref.shape, F32)
    far = far_field(plan, far_ref, tables, target)
    near_field(plan, list_ref, src_ref, face_ref, rank_ref, row_ref, comp_ref, part_ref)
    return [act * (GRAV * (row_ref[c] + far[c])) for c in range(3)]


def lane_row(plan, level, bit):
    cut, _, _ = plan.place[level]
    lane = lax.broadcasted_iota(jnp.int32, (1, plan.size), 1)
    return jnp.where(lane == 1 + cut, shift_of(plan, level, bit), 0.0)


def square_row(acc):
    square = acc[0] * acc[0] + acc[1] * acc[1] + acc[2] * acc[2]
    return jnp.max(square, axis=0, keepdims=True)


def time_step_of(square):
    return ETA / jnp.sqrt(jnp.sqrt(square) + 1e-06)


def second_kernel(plan, *refs):
    base_ref, list_ref, far_ref = refs[:3]
    near_refs = refs[3:6]
    extra = plan.levels - 3
    moment_refs = refs[6 : 6 + extra]
    acc_ref, max_ref, mom_ref = refs[6 + extra : 9 + extra]
    send_refs = refs[9 + extra : 12 + extra]
    src_ref, face_ref, *scratch = refs[12 + extra :]
    rows = plan.rows
    bits = device_bits(plan.levels)
    src_ref[...] = base_ref[pl.ds(0, 4)]
    tables = []
    others = list(moment_refs)
    for level in range(plan.levels):
        slot = plan.place[level][2]
        table = near_refs[slot][pl.ds(plan.row_t, rows), :] if slot >= 0 else others.pop(0)[...]
        tables.append(table + lane_row(plan, level, bits[level]))
    face = plan.face
    for slot in range(3):
        level = plan.near_level[slot]
        cut = plan.place[level][0]
        for c in range(3):
            value = near_refs[slot][pl.ds(c * face, face), :]
            if c == cut:
                value = value + shift_of(plan, level, bits[level])
            face_ref[slot, c, pl.ds(0, face), :] = value
        face_ref[slot, 3, pl.ds(0, face), :] = near_refs[slot][pl.ds(plan.row_m, face), :]
    act = base_ref[7]
    position = [base_ref[c] for c in range(3)]
    acc = forces(plan, act, position, tables, list_ref, far_ref, src_ref, face_ref, scratch)
    for c in range(3):
        acc_ref[c] = acc[c]
    max_ref[...] = square_row(acc)
    table = moment_table(base_ref[3], [position, [base_ref[4 + c] for c in range(3)], acc])
    mom_ref[...] = table
    for slot, ref in enumerate(send_refs):
        ref[pl.ds(plan.frows, rows), :] = table
        for s, row in enumerate(face_rows(plan, slot, bits[plan.near_level[slot]])):
            for c in range(3):
                ref[pl.ds(c * face + s, 1), :] = acc_ref[c, pl.ds(row, 1), :]


def third_kernel(plan, *refs):
    base_ref, list_ref, far_ref, acc_ref, max_ref = refs[:5]
    near_refs = refs[5:8]
    send_refs = refs[8:11]
    extra = plan.levels - 3
    moment_refs = refs[11 : 11 + extra]
    pos_ref, out_ref, square_ref, step_ref = refs[11 + extra : 15 + extra]
    src_ref, face_ref, moved_ref, *scratch = refs[15 + extra :]
    rows, size = plan.rows, plan.size
    bits = device_bits(plan.levels)
    step = time_step_of(jnp.max(max_ref[...], axis=(0, 1), keepdims=True))
    step_ref[...] = jnp.broadcast_to(step, step_ref.shape)
    dt = jnp.broadcast_to(step, (8, size))
    wide = jnp.broadcast_to(step, (rows, size))
    position = []
    for c in range(3):
        moved = base_ref[c] + (base_ref[4 + c] + acc_ref[c] * wide) * wide
        pos_ref[c] = moved
        src_ref[c] = moved
        position.append(moved)
    src_ref[3] = base_ref[3]
    lane = lax.broadcasted_iota(jnp.int32, (rows, size), 1)
    tables = []
    others = list(moment_refs)
    for level in range(plan.levels):
        slot = plan.place[level][2]
        table = send_refs[slot][pl.ds(plan.frows, rows), :] if slot >= 0 else others.pop(0)[...]
        total = None
        for k in range(4, -1, -1):
            part = pltpu.roll(table, size - k * STEP, 1) if k else table
            total = part if total is None else total * wide + part
        tables.append(jnp.where(lane < 10, total, 0.0) + lane_row(plan, level, bits[level]))
    face = plan.face
    frows = plan.frows
    fwide = jnp.broadcast_to(step, (frows, size))
    for slot in range(3):
        level = plan.near_level[slot]
        cut = plan.place[level][0]
        near = near_refs[slot]
        moved_ref[...] = (
            near[pl.ds(0, frows), :]
            + (near[pl.ds(plan.row_u, frows), :] + send_refs[slot][pl.ds(0, frows), :] * fwide)
            * fwide
        )
        for c in range(3):
            value = moved_ref[pl.ds(c * face, face), :]
            if c == cut:
                value = value + shift_of(plan, level, bits[level])
            face_ref[slot, c, pl.ds(0, face), :] = value
        face_ref[slot, 3, pl.ds(0, face), :] = near[pl.ds(plan.row_m, face), :]
    act = base_ref[7]
    acc = forces(plan, act, position, tables, list_ref, far_ref, src_ref, face_ref, scratch)
    for c in range(3):
        out_ref[c] = acc[c]
    square_ref[...] = square_row(acc)


def last_kernel(plan, max_ref, vel_ref, base_ref, pos_ref, first_ref, acc_ref, step_ref,
                pos_out, vel_out, acc_out, steps_out, work_ref):
    rows, size = plan.rows, plan.size
    second = time_step_of(jnp.max(max_ref[...], axis=(0, 1), keepdims=True))
    one = step_ref[...]
    lane = lax.broadcasted_iota(jnp.int32, (1, size), 1)
    steps_out[...] = jnp.where(lane == 0, one, second)
    first = jnp.broadcast_to(one[:, :1], (rows, size))
    wide = jnp.broadcast_to(second, (rows, size))
    for c in range(3):
        kick = acc_ref[c] * wide
        before = first_ref[c] * first
        work_ref[0, c] = pos_ref[c] + (base_ref[4 + c] + before + kick) * wide
        work_ref[1, c] = before
        work_ref[2, c] = kick
    for t in range(plan.tiles):
        lanes = pl.ds(t * size, size)
        for c in range(3):
            pos_out[pl.ds(c, 1), lanes] = work_ref[0, c, pl.ds(t, 1), :]
            vel_out[pl.ds(c, 1), lanes] = (
                vel_ref[pl.ds(c, 1), lanes] + work_ref[1, c, pl.ds(t, 1), :]
            ) + work_ref[2, c, pl.ds(t, 1), :]
            acc_out[pl.ds(c, 1), lanes] = acc_ref[c, pl.ds(t, 1), :]


def vmem():
    return pl.BlockSpec(memory_space=pltpu.VMEM)


def smem():
    return pl.BlockSpec(memory_space=pltpu.SMEM)


def call(kernel, outs, scratch, specs, name):
    return pl.pallas_call(
        kernel,
        out_shape=[jax.ShapeDtypeStruct(shape, F32) for shape in outs],
        in_specs=specs,
        out_specs=[vmem() for _ in outs],
        scratch_shapes=[pltpu.VMEM(shape, F32) for shape in scratch],
        name=name,
    )


def exchange(plan, block, bits):
    flip = sum(1 << bit for bit in bits)
    return lax.ppermute(block, AXES, [(i, i ^ flip) for i in range(plan.devices)])


def body(mesh, offsets, velocities, masses, active, near_local, near_remote, far_list):
    tiles, kl = near_local.shape
    kn = near_remote.shape[2]
    levels, km = far_list.shape[1:]
    size = masses.shape[0] // tiles
    plan = Plan(mesh, tiles, size, levels, km, kl, kn)
    rows, near_rows = plan.rows, plan.near_rows
    whole = (3, rows, size)
    extra = levels - 3
    active2 = active.reshape(tiles, size)
    base, moments, *near = call(
        functools.partial(first_kernel, plan),
        [(8, rows, size), (rows, size)] + [(near_rows, size)] * 3,
        [],
        [vmem()] * 4,
        "first",
    )(offsets, velocities, masses.reshape(tiles, size), active2)

    got_near = [None] * 3
    got_far = []
    for slot in range(3):
        got_near[slot] = exchange(plan, near[slot], [plan.near_level[slot]])
    for level in range(levels):
        if plan.place[level][2] < 0:
            got_far.append(exchange(plan, moments, [level]))

    counts = jnp.sum(active2, axis=1)
    lists = jnp.concatenate(
        [
            jnp.concatenate([near_local, near_remote.reshape(tiles, 3 * kn)], axis=1).reshape(-1),
            counts,
            jnp.max(counts)[None],
        ]
    )
    far_ids = far_list.reshape(tiles, levels * km)
    far_ids = jnp.concatenate(
        [far_ids, jnp.zeros((rows - tiles, levels * km), jnp.int32)], axis=0
    )
    fast = FAST_GROUPS * 8
    scratch = [
        (4, rows, size),
        (3, 4, up8(plan.face), size),
        (rows, size),
        whole,
        (tiles, fast, size),
        (tiles, FAST_GROUPS, 3, 8, size),
    ]
    send_rows = plan.frows + rows
    acc, square, table, *send = call(
        functools.partial(second_kernel, plan),
        [whole, (1, size), (rows, size)] + [(send_rows, size)] * 3,
        scratch,
        [vmem(), smem()] + [vmem()] * (1 + levels),
        "second",
    )(base, lists, far_ids, *got_near, *got_far)

    got_send = [None] * 3
    got_table = {}
    best = square
    for stage in plan.stages:
        flips = [[bit] for bit in stage] + ([stage] if len(stage) > 1 else [])
        seen = [best]
        for flip in flips:
            slot = plan.place[flip[0]][2] if len(flip) == 1 else -1
            if len(flip) > 1:
                seen.append(exchange(plan, best, flip))
                continue
            data = send[slot] if slot >= 0 else table
            there = exchange(plan, jnp.concatenate([data, best], axis=0), flip)
            seen.append(there[data.shape[0] :])
            if slot >= 0:
                got_send[slot] = there
            else:
                got_table[flip[0]] = there
        best = functools.reduce(jnp.maximum, seen)
    moved, acc2, square2, step = call(
        functools.partial(third_kernel, plan),
        [whole, whole, (1, size), (1, size)],
        scratch[:2] + [(plan.frows, size)] + scratch[2:],
        [vmem(), smem()] + [vmem()] * (3 + 3 + 3 + extra),
        "third",
    )(
        base, lists, far_ids, acc, best, *got_near, *got_send,
        *[got_table[level][:rows] for level in range(levels) if plan.place[level][2] < 0],
    )
    spread = jnp.broadcast_to(square2[None], (plan.devices, 1, size))
    everyone = lax.all_to_all(spread, AXES, 0, 0).reshape(plan.devices, size)
    pos, vel, out, steps = call(
        functools.partial(last_kernel, plan),
        [offsets.shape, offsets.shape, offsets.shape, (1, size)],
        [(3, 3, rows, size)],
        [vmem()] * 7,
        "last",
    )(everyone, velocities, base, moved, acc, acc2, step)
    return pos, vel, out, steps[0, :SUBSTEPS]


def solution(mesh):
    parts = P(None, AXES)
    return jax.shard_map(
        functools.partial(body, mesh),
        mesh=mesh,
        in_specs=(parts, parts, P(AXES), P(AXES), P(AXES, None), P(AXES, None, None), P(AXES, None, None)),
        out_specs=(parts, parts, parts, P()),
        check_vma=False,
    )
```

time: 188 us -> 68.1 us (0.36)
  blocking collectives: 77.3 us -> 10.9 us
  other arithmetic: 59 us -> 3.39 us
  Pallas kernels: 0 us -> 22.8 us
  local copies, waits for them, and re-layouts: 26.1 us -> 7.77 us
  loops' own time: 5.31 us -> 0 us
  waiting for transfers between devices: 2.58 us -> 6.61 us
  between operations: 3.01 us -> 0.8 us
    pmax x2 -> x0, blocking collectives: 77.3 us -> none  [body(): largest = lax.pmax(local_largest, ('gx', 'gy', 'gz'))]
    reduce_sum x248 -> x1, other arithmetic: 37.3 us -> 0.11 us  [body(): counts = jnp.sum(active2, axis=1)]
    pallas_call x0 -> x4, Pallas kernels: none -> 22.8 us  [the longest x1 9.62 us: body(): call(functools.partial(third_kernel, plan), [whole, whole, (1, size), (1,...]
    all_to_all x0 -> x1, blocking collectives: none -> 10.9 us  [body(): everyone = lax.all_to_all(spread, AXES, 0, 0).reshape(plan.devices, size)]
    gather x16 -> x0, local copies, waits for them, and re-layouts: 8.75 us -> none  [the longest x6 3.46 us: body(): jnp.take(partner_bodies, face_index(cut_axis, face_coord, tile_grid), axi...]
    add x58 -> x0, other arithmetic: 7.42 us -> none  [the longest x54 7.12 us: far_field(): moments[4] * relative[0] + moments[7] * relative[1]]
    mul x173 -> x0, other arithmetic: 5.65 us -> none  [the longest x54 3.35 us: tile_force(): strength = sources[3][None, :] * inverse * inverse * inverse]
    sub x108 -> x0, local copies, waits for them, and re-layouts: 5.49 us -> none  [the longest x54 5.14 us: far_field(): relative = target[:, :, None] - moments[1:4, None, :]]
  transfers between devices with their start and end apart: 10 -> 12, of which waited for: 3 -> 3; matrix products, arithmetic and copies ran while one was open for 3% -> 6% of each run, Pallas kernels for 0% -> 0%
where the time goes in v1:
time: 68.1 us; the launch traced here: 67.7 us
  Pallas kernels  22.8 us (33%)
  starting transfers between devices  15.5 us (23%)
  blocking collectives  10.9 us (16%)
  local copies, waits for them, and re-layouts  7.77 us (11%)
  waiting for transfers between devices  6.61 us (10%)
  other arithmetic  3.39 us (5%)
  between operations  0.8 us (1%)
    ppermute x12, starting transfers between devices, exchange(): lax.ppermute(block, AXES, [(i, i ^ flip) for i in range(plan.devices)])  15.5 us
    all_to_all x1, blocking collectives, body(): everyone = lax.all_to_all(spread, AXES, 0, 0).reshape(plan.devices, size)  10.9 us
    pallas_call x1, Pallas kernels, body(): call(functools.partial(third_kernel, plan), [whole, whole, (1, size), (1,...  9.62 us
    pallas_call x1, Pallas kernels, body(): call(functools.partial(second_kernel, plan), [whole, (1, size), (rows, si...  9.48 us
    ppermute x12, waiting for transfers between devices, exchange(): lax.ppermute(block, AXES, [(i, i ^ flip) for i in range(plan.devices)])  6.61 us
    unnamed x37, local copies, waits for them, and re-layouts  5.13 us
    pallas_call x1, Pallas kernels, body(): call(functools.partial(last_kernel, plan), [offsets.shape, offsets.shape,...  1.89 us
    pallas_call x1, Pallas kernels, body(): call(functools.partial(first_kernel, plan), [(8, rows, size), (rows, size...  1.78 us
  transfers between devices with their start and end apart: 12, of which 3 were waited for; matrix products, arithmetic and copies ran while one was open for 6% of the time, Pallas kernels for 0%

profile of v1, /device:TPU:0, one launch (start us, length us, event | category | flops | bytes accessed | tf_op | source)
XLA Modules:
  0.0 67.7 jit_solution(5216265207725376668)
XLA Ops:
  0.6 1.8 %first.1 = (f32[8,32,128]{2,1,0:T(8,128)}, f32[32,128]{1,0:T(8,128)}, f32[112,128]{1,0:T(8,128)}, f32[112,128]{1,0:T(8,128)}, f32[112,128]{1,0:T(8,128)}) custom-call(f32[3,3456]{1,0:T(4,128)} %off_ref.1, f32[3,3456]{1,0:T(4,128)} %vel_ref.3, f32[27,128]{1,0:T(8,128)} %bitcast.15, s32[27,128]{1,0:T(8,128)} %bitcast.13), custom_call_target="tpu_custom_call" | custom-call | tf_op jit(solution)/shard_map/first/pallas_call | solution.py:494
  2.4 3.0 %collective-permute-start.4 = (f32[32,128]{1,0:T(8,128)}, f32[32,128]{1,0:T(8,128)S(1)}, u32[]{:S(2)}, u32[]{:S(2)}) collective-permute-start(f32[32,128]{1,0:T(8,128)} %get-tuple-element.27), channel_id=1, source_target_pairs={{0,16},{1,17},{2,18},{3,19},{4,20},{5,21},{6,22},{7,23},{8,24},{9,... | collective-permute-start | bytes 49160 | tf_op jit(solution)/shard_map/ppermute | solution.py:481
  5.4 2.6 %collective-permute-start.3 = (f32[32,128]{1,0:T(8,128)}, f32[32,128]{1,0:T(8,128)S(1)}, u32[]{:S(2)}, u32[]{:S(2)}) collective-permute-start(f32[32,128]{1,0:T(8,128)} %get-tuple-element.27), channel_id=1, source_target_pairs={{0,2},{1,3},{2,0},{3,1},{4,6},{5,7},{6,4},{7,5},{8,10},{9,11},{10,... | collective-permute-start | bytes 49160 | tf_op jit(solution)/shard_map/ppermute | solution.py:481
  8.0 1.6 %collective-permute-start = (f32[112,128]{1,0:T(8,128)}, f32[112,128]{1,0:T(8,128)S(1)}, u32[]{:S(2)}, u32[]{:S(2)}) collective-permute-start(f32[112,128]{1,0:T(8,128)} %get-tuple-element.24), channel_id=1, source_target_pairs={{0,1},{1,0},{2,3},{3,2},{4,5},{5,4},{6,7},{7,6},{8,9},{9,8},{10,11... | collective-permute-start | bytes 172040 | tf_op jit(solution)/shard_map/ppermute | solution.py:481
  9.6 1.5 %collective-permute-start.1 = (f32[112,128]{1,0:T(8,128)}, f32[112,128]{1,0:T(8,128)S(1)}, u32[]{:S(2)}, u32[]{:S(2)}) collective-permute-start(f32[112,128]{1,0:T(8,128)} %get-tuple-element.25), channel_id=1, source_target_pairs={{0,4},{1,5},{2,6},{3,7},{4,0},{5,1},{6,2},{7,3},{8,12},{9,13},{10,... | collective-permute-start | bytes 172040 | tf_op jit(solution)/shard_map/ppermute | solution.py:481
  11.2 0.6 copy-done.14
  11.8 0.7 copy-done.15
  12.7 0.6 reduce_max.9
  13.3 1.3 %pad_add_fusion.1.refs_1_ = s32[163]{0:T(256)} fusion(s32[1]{0:T(128)} %bitcast.2, s32[27]{0:T(128)S(1)} %bitcast_reduce_fusion, s32[135]{0:T(256)S(1)} %reshape.32), kind=kLoop, calls=%fused_computation.7 | loop fusion | flops 326 | bytes 1304 | tf_op jit(solution)/shard_map/concatenate | solution.py:511
  14.7 0.6 concatenate.26.refs_2_
  15.4 0.5 copy-done.10
  16.0 9.5 %second.1 = (f32[3,32,128]{2,1,0:T(8,128)}, f32[1,128]{1,0:T(1,128)}, f32[32,128]{1,0:T(8,128)}, f32[64,128]{1,0:T(8,128)}, f32[64,128]{1,0:T(8,128)}, /*index=5*/f32[64,128]{1,0:T(8,128)}) custom-call(f32[8,32,128]{2,1,0:T(8,128)} %get-tuple-element.23.refs_0_.base_ref, s32[163]{0:T(256)} %pad_add_fusion.1.refs_1_, s32[32,10]{1,0:T(8,128)} %concatenate.26.refs_2_, ...), custom_call_target="tpu_custom_call" | custom-call | tf_op jit(solution)/shard_map/second/pallas_call | solution.py:532
  25.5 0.7 copy-done.13
  26.2 0.8 %pad_maximum_fusion = f32[65,128]{1,0:T(8,128)S(1)} fusion(f32[1,128]{1,0:T(1,128)S(1)} %copy-done.13, f32[64,128]{1,0:T(8,128)} %get-tuple-element.30), kind=kLoop, calls=%fused_computation | loop fusion | flops 8320 | bytes 66560 | tf_op jit(solution)/shard_map/concatenate | solution.py:552
  27.8 3.6 %collective-permute-start.7 = (f32[1,128]{1,0:T(1,128)S(1)}, f32[1,128]{1,0:T(1,128)S(1)}, u32[]{:S(2)}, u32[]{:S(2)}) collective-permute-start(f32[1,128]{1,0:T(1,128)S(1)} %copy-done.13), channel_id=1, source_target_pairs={{0,3},{1,2},{2,1},{3,0},{4,7},{5,6},{6,5},{7,4},{8,11},{9,10},{10,... | collective-permute-start | bytes 1544 | tf_op jit(solution)/shard_map/ppermute | solution.py:481
  31.4 1.8 %collective-permute-done.7 = f32[1,128]{1,0:T(1,128)S(1)} collective-permute-done((f32[1,128]{1,0:T(1,128)S(1)}, f32[1,128]{1,0:T(1,128)S(1)}, u32[]{:S(2)}, u32[]{:S(2)}) %collective-permute-start.7) | collective-permute-done | bytes 544 | tf_op jit(solution)/shard_map/ppermute | solution.py:481
  33.2 0.6 copy-done.5
  33.8 0.5 collective-permute-start.8
  34.3 3.4 %collective-permute-done.8.refs_9_ = f32[65,128]{1,0:T(8,128)S(1)} collective-permute-done((f32[65,128]{1,0:T(8,128)S(1)}, f32[65,128]{1,0:T(8,128)S(1)}, u32[]{:S(2)}, u32[]{:S(2)}) %collective-permute-start.8) | collective-permute-done | bytes 33312 | tf_op jit(solution)/shard_map/ppermute | solution.py:481
  37.8 0.6 copy-done.7
  38.4 0.6 collective-permute-start.10
  38.9 1.3 %collective-permute-start.11 = (f32[1,128]{1,0:T(1,128)S(1)}, f32[1,128]{1,0:T(1,128)S(1)}, u32[]{:S(2)}, u32[]{:S(2)}) collective-permute-start(f32[1,128]{1,0:T(1,128)S(1)} %slice_maximum_fusion.2), channel_id=1, source_target_pairs={{0,24},{1,25},{2,26},{3,27},{4,28},{5,29},{6,30},{7,31},{8,16},{9,... | collective-permute-start | bytes 1544 | tf_op jit(solution)/shard_map/ppermute | solution.py:481
  40.2 0.6 slice.37.refs_11_
  40.8 1.4 %collective-permute-done.10 = f32[33,128]{1,0:T(8,128)S(1)} collective-permute-done((f32[33,128]{1,0:T(8,128)S(1)}, f32[33,128]{1,0:T(8,128)S(1)}, u32[]{:S(2)}, u32[]{:S(2)}) %collective-permute-start.10) | collective-permute-done | bytes 16928 | tf_op jit(solution)/shard_map/ppermute | solution.py:481
  42.2 0.6 slice.38.refs_12_
  42.8 0.5 fusion.refs_4_
  43.4 9.6 %third.1 = (f32[3,32,128]{2,1,0:T(8,128)}, f32[3,32,128]{2,1,0:T(8,128)}, f32[1,128]{1,0:T(1,128)}, f32[1,128]{1,0:T(1,128)}) custom-call(f32[8,32,128]{2,1,0:T(8,128)} %get-tuple-element.23.refs_0_.base_ref, s32[163]{0:T(256)} %pad_add_fusion.1.refs_1_, s32[32,10]{1,0:T(8,128)} %concatenate.26.refs_2_, f32[3,32,128]{2,1,0:T(8,128)} %get-tuple-element.28.refs_3_.first_ref, ...), custom_call_target="tpu_custom_call" | custom-call | tf_op jit(solution)/shard_map/third/pallas_call | solution.py:559
  53.1 0.7 copy-done.16
  53.8 10.9 %all_to_all.5 = f32[32,1,128]{2,1,0:T(1,128)} all-to-all(f32[32,1,128]{2,1,0:T(1,128)S(1)} %broadcast_in_dim.14), channel_id=1, replica_groups=mesh['gx'=4,'gy'=2,'gz'=4] {'gx','gy','gz'}, dimensions={0} | all-to-all | bytes 32768 | tf_op jit(solution)/shard_map/all_to_all | solution.py:570
  64.7 1.9 %last.1 = (f32[3,3456]{1,0:T(4,128)}, f32[3,3456]{1,0:T(4,128)}, f32[3,3456]{1,0:T(4,128)}, f32[1,128]{1,0:T(1,128)}) custom-call(f32[32,128]{1,0:T(8,128)} %bitcast.14, f32[3,3456]{1,0:T(4,128)} %vel_ref.3, f32[8,32,128]{2,1,0:T(8,128)} %get-tuple-element.23.refs_0_.base_ref, f32[3,32,128]{2,1,0:T(8,128)} %get-tuple-element.35.pos_ref, ...), custom_call_target="tpu_custom_call" | custom-call | tf_op jit(solution)/shard_map/last/pallas_call | solution.py:571
  66.6 0.7 copy-done.17
  67.2 0.5 slice_bitcast_fusion
  (55 shorter events, 1.6 us)
Async XLA Ops:
  0.6 10.4 %copy-start.3 = (s32[3456]{0:T(1024)S(1)}, s32[3456]{0:T(1024)}, u32[]{:S(2)}) copy-start(s32[3456]{0:T(1024)} %param.10) | copy-start | bytes 41476
  2.4 12.9 %collective-permute-start.4 = (f32[32,128]{1,0:T(8,128)}, f32[32,128]{1,0:T(8,128)S(1)}, u32[]{:S(2)}, u32[]{:S(2)}) collective-permute-start(f32[32,128]{1,0:T(8,128)} %get-tuple-element.27), channel_id=1, source_target_pairs={{0,16},{1,17},{2,18},{3,19},{4,20},{5,21},{6,22},{7,23},{8,24},{9,... | collective-permute-start | bytes 49160 | tf_op jit(solution)/shard_map/ppermute | solution.py:481
  5.4 9.9 %collective-permute-start.3 = (f32[32,128]{1,0:T(8,128)}, f32[32,128]{1,0:T(8,128)S(1)}, u32[]{:S(2)}, u32[]{:S(2)}) collective-permute-start(f32[32,128]{1,0:T(8,128)} %get-tuple-element.27), channel_id=1, source_target_pairs={{0,2},{1,3},{2,0},{3,1},{4,6},{5,7},{6,4},{7,5},{8,10},{9,11},{10,... | collective-permute-start | bytes 49160 | tf_op jit(solution)/shard_map/ppermute | solution.py:481
  8.0 7.3 %collective-permute-start = (f32[112,128]{1,0:T(8,128)}, f32[112,128]{1,0:T(8,128)S(1)}, u32[]{:S(2)}, u32[]{:S(2)}) collective-permute-start(f32[112,128]{1,0:T(8,128)} %get-tuple-element.24), channel_id=1, source_target_pairs={{0,1},{1,0},{2,3},{3,2},{4,5},{5,4},{6,7},{7,6},{8,9},{9,8},{10,11... | collective-permute-start | bytes 172040 | tf_op jit(solution)/shard_map/ppermute | solution.py:481
  9.6 5.8 %collective-permute-start.1 = (f32[112,128]{1,0:T(8,128)}, f32[112,128]{1,0:T(8,128)S(1)}, u32[]{:S(2)}, u32[]{:S(2)}) collective-permute-start(f32[112,128]{1,0:T(8,128)} %get-tuple-element.25), channel_id=1, source_target_pairs={{0,4},{1,5},{2,6},{3,7},{4,0},{5,1},{6,2},{7,3},{8,12},{9,13},{10,... | collective-permute-start | bytes 172040 | tf_op jit(solution)/shard_map/ppermute | solution.py:481
  11.1 0.7 %copy-start.14 = (s32[27,3,1]{0,2,1:T(1,128)S(1)}, s32[27,3,1]{0,2,1:T(1,128)}, u32[]{:S(2)}) copy-start(s32[27,3,1]{0,2,1:T(1,128)} %param.12) | copy-start | bytes 976
  11.1 4.3 %collective-permute-start.2 = (f32[112,128]{1,0:T(8,128)}, f32[112,128]{1,0:T(8,128)S(1)}, u32[]{:S(2)}, u32[]{:S(2)}) collective-permute-start(f32[112,128]{1,0:T(8,128)} %get-tuple-element.26), channel_id=1, source_target_pairs={{0,8},{1,9},{2,10},{3,11},{4,12},{5,13},{6,14},{7,15},{8,0},{9,1},... | collective-permute-start | bytes 172040 | tf_op jit(solution)/shard_map/ppermute | solution.py:481
  11.8 0.7 %copy-start.15 = (s32[27,2]{0,1:T(2,128)S(1)}, s32[27,2]{0,1:T(2,128)}, u32[]{:S(2)}) copy-start(s32[27,2]{0,1:T(2,128)} %param.11) | copy-start | bytes 652
  12.6 2.0 %copy-start.12 = (s32[27,5,2]{0,2,1:T(2,128)S(1)}, s32[27,5,2]{0,2,1:T(2,128)}, u32[]{:S(2)}) copy-start(s32[27,5,2]{0,2,1:T(2,128)} %param.13) | copy-start | bytes 3244
  15.3 0.6 copy-start.10
  15.3 0.6 copy-start.11
  15.3 0.6 copy-start
  15.4 0.6 copy-start.1
  15.4 0.6 copy-start.2
  25.5 0.7 copy-start.13
  26.2 1.2 %copy-start.4 = (f32[32,128]{1,0:T(8,128)S(1)}, f32[32,128]{1,0:T(8,128)}, u32[]{:S(2)}) copy-start(f32[32,128]{1,0:T(8,128)} %get-tuple-element.31) | copy-start | bytes 49156
  26.9 6.3 %copy-start.9 = (f32[64,128]{1,0:T(8,128)S(1)}, f32[64,128]{1,0:T(8,128)}, u32[]{:S(2)}) copy-start(f32[64,128]{1,0:T(8,128)} %get-tuple-element.32) | copy-start | bytes 98308
  26.9 6.2 %collective-permute-start.5 = (f32[65,128]{1,0:T(8,128)S(1)}, f32[65,128]{1,0:T(8,128)S(1)}, u32[]{:S(2)}, u32[]{:S(2)}) collective-permute-start(f32[65,128]{1,0:T(8,128)S(1)} %pad_maximum_fusion), channel_id=1, source_target_pairs={{0,1},{1,0},{2,3},{3,2},{4,5},{5,4},{6,7},{7,6},{8,9},{9,8},{10,11... | collective-permute-start | bytes 99848 | tf_op jit(solution)/shard_map/ppermute | solution.py:481
  27.4 5.8 %collective-permute-start.6 = (f32[33,128]{1,0:T(8,128)S(1)}, f32[33,128]{1,0:T(8,128)S(1)}, u32[]{:S(2)}, u32[]{:S(2)}) collective-permute-start(f32[33,128]{1,0:T(8,128)S(1)} %pad_maximum_fusion.4), channel_id=1, source_target_pairs={{0,2},{1,3},{2,0},{3,1},{4,6},{5,7},{6,4},{7,5},{8,10},{9,11},{10,... | collective-permute-start | bytes 50696 | tf_op jit(solution)/shard_map/ppermute | solution.py:481
  27.8 5.4 %collective-permute-start.7 = (f32[1,128]{1,0:T(1,128)S(1)}, f32[1,128]{1,0:T(1,128)S(1)}, u32[]{:S(2)}, u32[]{:S(2)}) collective-permute-start(f32[1,128]{1,0:T(1,128)S(1)} %copy-done.13), channel_id=1, source_target_pairs={{0,3},{1,2},{2,1},{3,0},{4,7},{5,6},{6,5},{7,4},{8,11},{9,10},{10,... | collective-permute-start | bytes 1544 | tf_op jit(solution)/shard_map/ppermute | solution.py:481
  33.2 0.6 copy-start.5
  33.2 4.6 %copy-start.8 = (f32[64,128]{1,0:T(8,128)S(1)}, f32[64,128]{1,0:T(8,128)}, u32[]{:S(2)}) copy-start(f32[64,128]{1,0:T(8,128)} %get-tuple-element.33) | copy-start | bytes 98308
  33.8 4.0 %collective-permute-start.8 = (f32[65,128]{1,0:T(8,128)S(1)}, f32[65,128]{1,0:T(8,128)S(1)}, u32[]{:S(2)}, u32[]{:S(2)}) collective-permute-start(f32[65,128]{1,0:T(8,128)S(1)} %pad_maximum_fusion.1), channel_id=1, source_target_pairs={{0,4},{1,5},{2,6},{3,7},{4,0},{5,1},{6,2},{7,3},{8,12},{9,13},{10,... | collective-permute-start | bytes 99848 | tf_op jit(solution)/shard_map/ppermute | solution.py:481
  37.7 0.6 copy-start.7
  38.4 4.5 %collective-permute-start.9 = (f32[65,128]{1,0:T(8,128)S(1)}, f32[65,128]{1,0:T(8,128)S(1)}, u32[]{:S(2)}, u32[]{:S(2)}) collective-permute-start(f32[65,128]{1,0:T(8,128)S(1)} %pad_maximum_fusion.2), channel_id=1, source_target_pairs={{0,8},{1,9},{2,10},{3,11},{4,12},{5,13},{6,14},{7,15},{8,0},{9,1},... | collective-permute-start | bytes 99848 | tf_op jit(solution)/shard_map/ppermute | solution.py:481
  38.4 3.8 %collective-permute-start.10 = (f32[33,128]{1,0:T(8,128)S(1)}, f32[33,128]{1,0:T(8,128)S(1)}, u32[]{:S(2)}, u32[]{:S(2)}) collective-permute-start(f32[33,128]{1,0:T(8,128)S(1)} %pad_maximum_fusion.3), channel_id=1, source_target_pairs={{0,16},{1,17},{2,18},{3,19},{4,20},{5,21},{6,22},{7,23},{8,24},{9,... | collective-permute-start | bytes 50696 | tf_op jit(solution)/shard_map/ppermute | solution.py:481
  38.9 3.9 %collective-permute-start.11 = (f32[1,128]{1,0:T(1,128)S(1)}, f32[1,128]{1,0:T(1,128)S(1)}, u32[]{:S(2)}, u32[]{:S(2)}) collective-permute-start(f32[1,128]{1,0:T(1,128)S(1)} %slice_maximum_fusion.2), channel_id=1, source_target_pairs={{0,24},{1,25},{2,26},{3,27},{4,28},{5,29},{6,30},{7,31},{8,16},{9,... | collective-permute-start | bytes 1544 | tf_op jit(solution)/shard_map/ppermute | solution.py:481
  42.8 0.6 copy-start.6
  53.1 0.7 copy-start.16
  66.6 0.7 copy-start.17

commit v2 on v1

--- a/solution.py
+++ b/solution.py
@@ -15,6 +15,7 @@
 F32 = jnp.float32
 BF16 = jnp.bfloat16
 FAST_GROUPS = 6
+VMEM_BYTES = 16 * 2**20
 STEP = 16
 
 
@@ -142,7 +143,15 @@
     ]
 
 
-def first_kernel(plan, off_ref, vel_ref, mass_ref, act_ref, base_ref, mom_ref, *near_refs):
+def first_kernel(plan, *refs):
+    ins, (base_ref, mom_ref, id_ref), near_refs = refs[:5], refs[5:8], refs[8:11]
+    buffers, sems = refs[11:16], refs[16]
+    copies = [pltpu.make_async_copy(ins[i], buffers[i], sems.at[i]) for i in range(5)]
+    for copy in copies:
+        copy.start()
+    for copy in copies:
+        copy.wait()
+    off_ref, vel_ref, mass_ref, act_ref, far_ref = buffers
     tiles, rows, size, grid = plan.tiles, plan.rows, plan.size, plan.grid
     tile = lax.broadcasted_iota(jnp.int32, (rows, size), 0)
     base_ref[...] = jnp.zeros(base_ref.shape, F32)
@@ -161,30 +170,39 @@
         value = jnp.where(inside, base_ref[c] + corners[c].astype(F32), 0.0)
         base_ref[c] = value
         position.append(value)
-        base_ref[4 + c] = base_ref[4 + c] * act
     mass = jnp.where(inside, base_ref[3], 1.0)
     base_ref[3] = mass
     table = moment_table(mass, [position])
     mom_ref[...] = table
+    lists = plan.levels * plan.km
+    flat = jnp.concatenate(
+        [far_ref[level].astype(F32) for level in range(plan.levels)]
+        + [jnp.zeros((up8(lists) - lists, tiles), F32)] * (lists % 8 > 0),
+        axis=0,
+    )
+    id_ref[pl.ds(0, tiles), pl.ds(0, up8(lists))] = jnp.transpose(flat).astype(jnp.int32)
     bits = device_bits(plan.levels)
     for slot, ref in enumerate(near_refs):
         ref[pl.ds(plan.row_t, rows), :] = table
         for s, row in enumerate(face_rows(plan, slot, bits[plan.near_level[slot]])):
             for c in range(3):
                 ref[pl.ds(c * plan.face + s, 1), :] = base_ref[c, pl.ds(row, 1), :]
-                ref[pl.ds(plan.row_u + c * plan.face + s, 1), :] = base_ref[4 + c, pl.ds(row, 1), :]
+                ref[pl.ds(plan.row_u + c * plan.face + s, 1), :] = (
+                    base_ref[4 + c, pl.ds(row, 1), :] * base_ref[7, pl.ds(row, 1), :]
+                )
             ref[pl.ds(plan.row_m + s, 1), :] = base_ref[3, pl.ds(row, 1), :]
 
 
 def far_field(plan, far_ref, tables, target):
     rows, size = plan.rows, plan.size
     cell = lax.broadcasted_iota(jnp.int32, (rows, rows), 1)
+    far_ids = far_ref[...]
     total = [jnp.zeros((rows, size), F32) for _ in range(3)]
     for level in range(plan.levels):
         parts = split3(tables[level])
         for k in range(plan.km):
             where = level * plan.km + k
-            pick = jnp.where(far_ref[:, pl.ds(where, 1)] == cell, 1.0, 0.0).astype(BF16)
+            pick = jnp.where(far_ids[:, where : where + 1] == cell, 1.0, 0.0).astype(BF16)
             got = dot_nn(pick, parts[0]) + dot_nn(pick, parts[1]) + dot_nn(pick, parts[2])
             q = [jnp.broadcast_to(got[:, p : p + 1], (rows, size)) for p in range(10)]
             r = [target[c] - q[1 + c] for c in range(3)]
@@ -229,11 +247,12 @@
     def source_rows(t):
         found = []
         for s in range(per_tile):
-            index = list_ref[t * per_tile + s]
             if s < kl:
+                index = list_ref[0][s, t]
                 found.append([src_ref[c, pl.ds(index, 1), :] for c in range(4)])
             else:
                 slot = (s - kl) // kn
+                index = list_ref[1][slot, (s - kl) % kn, t]
                 found.append([face_ref[slot, c, pl.ds(index, 1), :] for c in range(4)])
         return found
 
@@ -278,7 +297,7 @@
     lax.fori_loop(0, tiles, body, 0)
     scatter(last)
 
-    @pl.when(list_ref[tiles * per_tile + tiles] > fast)
+    @pl.when(jnp.max(rank_ref[...]) >= fast)
     def _():
         def tile_rest(t, carry):
             def group(g, inner):
@@ -291,7 +310,7 @@
                     row_ref[c, pl.ds(t, 1), :] = old + jnp.sum(value, axis=0, keepdims=True)
                 return inner
 
-            groups = (list_ref[tiles * per_tile + t] + 7) // 8
+            groups = (jnp.max(rank_ref[pl.ds(t, 1), :]).astype(jnp.int32) + 8) // 8
             lax.fori_loop(FAST_GROUPS, groups, group, 0)
             return carry
 
@@ -304,7 +323,21 @@
     return jnp.where(bit == 0, span, -span).astype(F32)
 
 
-def forces(plan, act, target, tables, list_ref, far_ref, src_ref, face_ref, scratch):
+def lists_start(ins, scratch):
+    outs, sems = scratch[:2], scratch[2]
+    copies = [pltpu.make_async_copy(ins[i], outs[i], sems.at[i]) for i in range(2)]
+    for copy in copies:
+        copy.start()
+
+    def arrived():
+        for copy in copies:
+            copy.wait()
+        return outs
+
+    return arrived
+
+
+def forces(plan, act, target, tables, arrived, far_ref, src_ref, face_ref, scratch):
     rank_ref, row_ref, comp_ref, part_ref = scratch
     rows, size = plan.rows, plan.size
     below = lax.broadcasted_iota(jnp.int32, (size, size), 0) < lax.broadcasted_iota(
@@ -314,7 +347,7 @@
     rank_ref[...] = jnp.where(act > 0, rank, -1.0)
     row_ref[...] = jnp.zeros(row_ref.shape, F32)
     far = far_field(plan, far_ref, tables, target)
-    near_field(plan, list_ref, src_ref, face_ref, rank_ref, row_ref, comp_ref, part_ref)
+    near_field(plan, arrived(), src_ref, face_ref, rank_ref, row_ref, comp_ref, part_ref)
     return [act * (GRAV * (row_ref[c] + far[c])) for c in range(3)]
 
 
@@ -334,13 +367,14 @@
 
 
 def second_kernel(plan, *refs):
-    base_ref, list_ref, far_ref = refs[:3]
-    near_refs = refs[3:6]
+    arrived, refs = lists_start(refs[:2], refs[-10:-7]), refs[2:]
+    base_ref, far_ref = refs[:2]
+    near_refs = refs[2:5]
     extra = plan.levels - 3
-    moment_refs = refs[6 : 6 + extra]
-    acc_ref, max_ref, mom_ref = refs[6 + extra : 9 + extra]
-    send_refs = refs[9 + extra : 12 + extra]
-    src_ref, face_ref, *scratch = refs[12 + extra :]
+    moment_refs = refs[5 : 5 + extra]
+    acc_ref, max_ref, mom_ref = refs[5 + extra : 8 + extra]
+    send_refs = refs[8 + extra : 11 + extra]
+    src_ref, face_ref, _, *scratch = refs[-7:]
     rows = plan.rows
     bits = device_bits(plan.levels)
     src_ref[...] = base_ref[pl.ds(0, 4)]
@@ -362,11 +396,11 @@
         face_ref[slot, 3, pl.ds(0, face), :] = near_refs[slot][pl.ds(plan.row_m, face), :]
     act = base_ref[7]
     position = [base_ref[c] for c in range(3)]
-    acc = forces(plan, act, position, tables, list_ref, far_ref, src_ref, face_ref, scratch)
+    acc = forces(plan, act, position, tables, arrived, far_ref, src_ref, face_ref, scratch)
     for c in range(3):
         acc_ref[c] = acc[c]
     max_ref[...] = square_row(acc)
-    table = moment_table(base_ref[3], [position, [base_ref[4 + c] for c in range(3)], acc])
+    table = moment_table(base_ref[3], [position, [base_ref[4 + c] * act for c in range(3)], acc])
     mom_ref[...] = table
     for slot, ref in enumerate(send_refs):
         ref[pl.ds(plan.frows, rows), :] = table
@@ -376,13 +410,14 @@
 
 
 def third_kernel(plan, *refs):
-    base_ref, list_ref, far_ref, acc_ref, max_ref = refs[:5]
-    near_refs = refs[5:8]
-    send_refs = refs[8:11]
+    arrived, refs = lists_start(refs[:2], refs[-10:-7]), refs[2:]
+    base_ref, far_ref, acc_ref, max_ref = refs[:4]
+    near_refs = refs[4:7]
+    send_refs = refs[7:10]
     extra = plan.levels - 3
-    moment_refs = refs[11 : 11 + extra]
-    pos_ref, out_ref, square_ref, step_ref = refs[11 + extra : 15 + extra]
-    src_ref, face_ref, moved_ref, *scratch = refs[15 + extra :]
+    moment_refs = refs[10 : 10 + extra]
+    pos_ref, out_ref, square_ref, step_ref = refs[10 + extra : 14 + extra]
+    src_ref, face_ref, moved_ref, *scratch = refs[-7:]
     rows, size = plan.rows, plan.size
     bits = device_bits(plan.levels)
     step = time_step_of(jnp.max(max_ref[...], axis=(0, 1), keepdims=True))
@@ -390,8 +425,9 @@
     dt = jnp.broadcast_to(step, (8, size))
     wide = jnp.broadcast_to(step, (rows, size))
     position = []
+    act = base_ref[7]
     for c in range(3):
-        moved = base_ref[c] + (base_ref[4 + c] + acc_ref[c] * wide) * wide
+        moved = base_ref[c] + (base_ref[4 + c] * act + acc_ref[c] * wide) * wide
         pos_ref[c] = moved
         src_ref[c] = moved
         position.append(moved)
@@ -425,35 +461,31 @@
                 value = value + shift_of(plan, level, bits[level])
             face_ref[slot, c, pl.ds(0, face), :] = value
         face_ref[slot, 3, pl.ds(0, face), :] = near[pl.ds(plan.row_m, face), :]
-    act = base_ref[7]
-    acc = forces(plan, act, position, tables, list_ref, far_ref, src_ref, face_ref, scratch)
+    acc = forces(plan, act, position, tables, arrived, far_ref, src_ref, face_ref, scratch)
     for c in range(3):
         out_ref[c] = acc[c]
     square_ref[...] = square_row(acc)
 
 
-def last_kernel(plan, max_ref, vel_ref, base_ref, pos_ref, first_ref, acc_ref, step_ref,
+def last_kernel(plan, max_ref, base_ref, pos_ref, first_ref, acc_ref, step_ref,
                 pos_out, vel_out, acc_out, steps_out, work_ref):
     rows, size = plan.rows, plan.size
     second = time_step_of(jnp.max(max_ref[...], axis=(0, 1), keepdims=True))
     one = step_ref[...]
-    lane = lax.broadcasted_iota(jnp.int32, (1, size), 1)
-    steps_out[...] = jnp.where(lane == 0, one, second)
+    steps_out[0] = one[0, 0]
+    steps_out[1] = second[0, 0]
     first = jnp.broadcast_to(one[:, :1], (rows, size))
     wide = jnp.broadcast_to(second, (rows, size))
+    act = base_ref[7]
     for c in range(3):
-        kick = acc_ref[c] * wide
-        before = first_ref[c] * first
-        work_ref[0, c] = pos_ref[c] + (base_ref[4 + c] + before + kick) * wide
-        work_ref[1, c] = before
-        work_ref[2, c] = kick
+        velocity = base_ref[4 + c] + first_ref[c] * first + acc_ref[c] * wide
+        work_ref[0, c] = pos_ref[c] + velocity * act * wide
+        work_ref[1, c] = velocity
     for t in range(plan.tiles):
         lanes = pl.ds(t * size, size)
         for c in range(3):
             pos_out[pl.ds(c, 1), lanes] = work_ref[0, c, pl.ds(t, 1), :]
-            vel_out[pl.ds(c, 1), lanes] = (
-                vel_ref[pl.ds(c, 1), lanes] + work_ref[1, c, pl.ds(t, 1), :]
-            ) + work_ref[2, c, pl.ds(t, 1), :]
+            vel_out[pl.ds(c, 1), lanes] = work_ref[1, c, pl.ds(t, 1), :]
             acc_out[pl.ds(c, 1), lanes] = acc_ref[c, pl.ds(t, 1), :]
 
 
@@ -461,19 +493,32 @@
     return pl.BlockSpec(memory_space=pltpu.VMEM)
 
 
+def hbm():
+    return pl.BlockSpec(memory_space=pltpu.HBM)
+
+
 def smem():
     return pl.BlockSpec(memory_space=pltpu.SMEM)
 
 
-def call(kernel, outs, scratch, specs, name):
+def call(kernel, outs, scratch, specs, name, out_specs=None):
     return pl.pallas_call(
         kernel,
-        out_shape=[jax.ShapeDtypeStruct(shape, F32) for shape in outs],
+        out_shape=outs,
         in_specs=specs,
-        out_specs=[vmem() for _ in outs],
-        scratch_shapes=[pltpu.VMEM(shape, F32) for shape in scratch],
+        out_specs=out_specs or [vmem() for _ in outs],
+        scratch_shapes=scratch,
+        compiler_params=pltpu.CompilerParams(vmem_limit_bytes=VMEM_BYTES),
         name=name,
     )
+
+
+def buffers(*shapes):
+    return [pltpu.VMEM(shape, F32) for shape in shapes]
+
+
+def floats(*shapes):
+    return [jax.ShapeDtypeStruct(shape, F32) for shape in shapes]
 
 
 def exchange(plan, block, bits):
@@ -490,14 +535,26 @@
     rows, near_rows = plan.rows, plan.near_rows
     whole = (3, rows, size)
     extra = levels - 3
-    active2 = active.reshape(tiles, size)
-    base, moments, *near = call(
+    base, moments, far_ids, *near = call(
         functools.partial(first_kernel, plan),
-        [(8, rows, size), (rows, size)] + [(near_rows, size)] * 3,
-        [],
-        [vmem()] * 4,
+        floats((8, rows, size), (rows, size))
+        + [jax.ShapeDtypeStruct((rows, size), jnp.int32)]
+        + floats(*[(near_rows, size)] * 3),
+        buffers(offsets.shape, velocities.shape, (tiles, size))
+        + [
+            pltpu.VMEM((tiles, size), jnp.int32),
+            pltpu.VMEM((levels, km, tiles), jnp.int32),
+            pltpu.SemaphoreType.DMA((5,)),
+        ],
+        [hbm()] * 5,
         "first",
-    )(offsets, velocities, masses.reshape(tiles, size), active2)
+    )(
+        offsets,
+        velocities,
+        masses.reshape(tiles, size),
+        active.reshape(tiles, size),
+        jnp.transpose(far_list, (1, 2, 0)),
+    )
 
     got_near = [None] * 3
     got_far = []
@@ -507,35 +564,29 @@
         if plan.place[level][2] < 0:
             got_far.append(exchange(plan, moments, [level]))
 
-    counts = jnp.sum(active2, axis=1)
-    lists = jnp.concatenate(
-        [
-            jnp.concatenate([near_local, near_remote.reshape(tiles, 3 * kn)], axis=1).reshape(-1),
-            counts,
-            jnp.max(counts)[None],
-        ]
-    )
-    far_ids = far_list.reshape(tiles, levels * km)
-    far_ids = jnp.concatenate(
-        [far_ids, jnp.zeros((rows - tiles, levels * km), jnp.int32)], axis=0
-    )
+    lists = (jnp.transpose(near_local), jnp.transpose(near_remote, (1, 2, 0)))
     fast = FAST_GROUPS * 8
     scratch = [
+        pltpu.SMEM((kl, tiles), jnp.int32),
+        pltpu.SMEM((3, kn, tiles), jnp.int32),
+        pltpu.SemaphoreType.DMA((2,)),
+    ] + buffers(
         (4, rows, size),
         (3, 4, up8(plan.face), size),
+        (plan.frows, size),
         (rows, size),
         whole,
         (tiles, fast, size),
         (tiles, FAST_GROUPS, 3, 8, size),
-    ]
+    )
     send_rows = plan.frows + rows
     acc, square, table, *send = call(
         functools.partial(second_kernel, plan),
-        [whole, (1, size), (rows, size)] + [(send_rows, size)] * 3,
+        floats(whole, (1, size), (rows, size), *[(send_rows, size)] * 3),
         scratch,
-        [vmem(), smem()] + [vmem()] * (1 + levels),
+        [hbm(), hbm()] + [vmem()] * (2 + levels),
         "second",
-    )(base, lists, far_ids, *got_near, *got_far)
+    )(*lists, base, far_ids, *got_near, *got_far)
 
     got_send = [None] * 3
     got_table = {}
@@ -558,24 +609,25 @@
         best = functools.reduce(jnp.maximum, seen)
     moved, acc2, square2, step = call(
         functools.partial(third_kernel, plan),
-        [whole, whole, (1, size), (1, size)],
-        scratch[:2] + [(plan.frows, size)] + scratch[2:],
-        [vmem(), smem()] + [vmem()] * (3 + 3 + 3 + extra),
+        floats(whole, whole, (1, size), (1, size)),
+        scratch,
+        [hbm(), hbm()] + [vmem()] * (4 + 3 + 3 + extra),
         "third",
     )(
-        base, lists, far_ids, acc, best, *got_near, *got_send,
+        *lists, base, far_ids, acc, best, *got_near, *got_send,
         *[got_table[level][:rows] for level in range(levels) if plan.place[level][2] < 0],
     )
     spread = jnp.broadcast_to(square2[None], (plan.devices, 1, size))
     everyone = lax.all_to_all(spread, AXES, 0, 0).reshape(plan.devices, size)
     pos, vel, out, steps = call(
         functools.partial(last_kernel, plan),
-        [offsets.shape, offsets.shape, offsets.shape, (1, size)],
-        [(3, 3, rows, size)],
-        [vmem()] * 7,
+        floats(offsets.shape, offsets.shape, offsets.shape, (SUBSTEPS,)),
+        buffers((2, 3, rows, size)),
+        [vmem()] * 6,
         "last",
-    )(everyone, velocities, base, moved, acc, acc2, step)
-    return pos, vel, out, steps[0, :SUBSTEPS]
+        [vmem(), vmem(), vmem(), smem()],
+    )(everyone, base, moved, acc, acc2, step)
+    return pos, vel, out, steps
 
 
 def solution(mesh):

time: 68.1 us -> 59.8 us (0.88)
  Pallas kernels: 22.8 us -> 17.6 us
  waiting for transfers between devices: 6.61 us -> 11.5 us
  other arithmetic: 3.39 us -> 0.05 us
  local copies, waits for them, and re-layouts: 7.77 us -> 4.44 us
  blocking collectives: 10.9 us -> 9.38 us
    pallas_call x4, Pallas kernels: 22.8 us -> 17.6 us  [the longest x1 8.13 us: body(): call(functools.partial(third_kernel, plan), floats(whole, whole, (1, size...]
    ppermute x12, waiting for transfers between devices: 6.61 us -> 11.5 us  [exchange(): lax.ppermute(block, AXES, [(i, i ^ flip) for i in range(plan.devices)])]
    all_to_all x1, blocking collectives: 10.9 us -> 9.38 us  [body(): everyone = lax.all_to_all(spread, AXES, 0, 0).reshape(plan.devices, size)]
    concatenate x2 -> x0, other arithmetic: 1.32 us -> none  [the longest x1 1.31 us: body(): jnp.concatenate([jnp.concatenate([near_local, near_remote.reshape(tiles,...]
    slice x2, local copies, waits for them, and re-layouts: 1.2 us -> 0.01 us  [body(): got_table[level][:rows]]
    concatenate x5, other arithmetic: 0.8 us -> 0.03 us  [body(): there = exchange(plan, jnp.concatenate([data, best], axis=0), flip)]
    unnamed x37 -> x14, local copies, waits for them, and re-layouts: 5.13 us -> 4.42 us
    concatenate x2 -> x0, local copies, waits for them, and re-layouts: 0.71 us -> none  [the longest x1 0.6 us: body(): jnp.concatenate([far_ids, jnp.zeros((rows - tiles, levels * km), jnp.int3...]
  transfers between devices with their start and end apart: 12 -> 12, of which waited for: 3 -> 4; matrix products, arithmetic and copies ran while one was open for 6% -> 0% of each run, Pallas kernels for 0% -> 0%
where the time goes in v2:
time: 59.8 us; the launch traced here: 59.4 us
  Pallas kernels  17.6 us (29%)
  starting transfers between devices  15.7 us (26%)
  waiting for transfers between devices  11.5 us (19%)
  blocking collectives  9.38 us (16%)
  local copies, waits for them, and re-layouts  4.44 us (7%)
  between operations  0.76 us (1%)
    ppermute x12, starting transfers between devices, exchange(): lax.ppermute(block, AXES, [(i, i ^ flip) for i in range(plan.devices)])  15.7 us
    ppermute x12, waiting for transfers between devices, exchange(): lax.ppermute(block, AXES, [(i, i ^ flip) for i in range(plan.devices)])  11.5 us
    all_to_all x1, blocking collectives, body(): everyone = lax.all_to_all(spread, AXES, 0, 0).reshape(plan.devices, size)  9.38 us
    pallas_call x1, Pallas kernels, body(): call(functools.partial(third_kernel, plan), floats(whole, whole, (1, size...  8.13 us
    pallas_call x1, Pallas kernels, body(): call(functools.partial(second_kernel, plan), floats(whole, (1, size), (ro...  8.05 us
    unnamed x14, local copies, waits for them, and re-layouts  4.42 us
  transfers between devices with their start and end apart: 12, of which 4 were waited for; matrix products, arithmetic and copies ran while one was open for 0% of the time, Pallas kernels for 0%

profile of v2, /device:TPU:0, one launch (start us, length us, event | category | flops | bytes accessed | tf_op | source)
XLA Modules:
  0.0 59.4 jit_solution(5422405659867944644)
XLA Ops:
  0.6 0.7 %copy-done.5 = s32[27,5,2]{0,2,1:T(2,128)S(1)} copy-done((s32[27,5,2]{0,2,1:T(2,128)S(1)}, s32[27,5,2]{0,2,1:T(2,128)}, u32[]{:S(2)}) %copy-start.5) | copy-done | bytes 1104
  1.3 0.8 %copy-done = f32[3,3456]{1,0:T(4,128)S(1)} copy-done((f32[3,3456]{1,0:T(4,128)S(1)}, f32[3,3456]{1,0:T(4,128)}, u32[]{:S(2)}) %copy-start) | copy-done | bytes 41496
  2.1 0.8 %copy-done.1 = f32[3,3456]{1,0:T(4,128)S(1)} copy-done((f32[3,3456]{1,0:T(4,128)S(1)}, f32[3,3456]{1,0:T(4,128)}, u32[]{:S(2)}) %copy-start.1) | copy-done | bytes 41496
  3.0 0.7 %copy-done.2 = f32[3456]{0:T(1024)S(1)} copy-done((f32[3456]{0:T(1024)S(1)}, f32[3456]{0:T(1024)}, u32[]{:S(2)}) %copy-start.2) | copy-done | bytes 13848
  3.7 0.7 %copy-done.3 = s32[3456]{0:T(1024)S(1)} copy-done((s32[3456]{0:T(1024)S(1)}, s32[3456]{0:T(1024)}, u32[]{:S(2)}) %copy-start.3) | copy-done | bytes 13848
  4.4 0.5 first.1
  4.9 3.1 %collective-permute-start = (f32[112,128]{1,0:T(8,128)S(1)}, f32[112,128]{1,0:T(8,128)S(1)}, u32[]{:S(2)}, u32[]{:S(2)}) collective-permute-start(f32[112,128]{1,0:T(8,128)S(1)} %get-tuple-element.22), channel_id=1, source_target_pairs={{0,1},{1,0},{2,3},{3,2},{4,5},{5,4},{6,7},{7,6},{8,9},{9,8},{10,11... | collective-permute-start | bytes 172040 | tf_op jit(solution)/shard_map/ppermute | solution.py:526
  8.0 1.5 %collective-permute-start.1 = (f32[112,128]{1,0:T(8,128)S(1)}, f32[112,128]{1,0:T(8,128)S(1)}, u32[]{:S(2)}, u32[]{:S(2)}) collective-permute-start(f32[112,128]{1,0:T(8,128)S(1)} %get-tuple-element.23), channel_id=1, source_target_pairs={{0,4},{1,5},{2,6},{3,7},{4,0},{5,1},{6,2},{7,3},{8,12},{9,13},{10,... | collective-permute-start | bytes 172040 | tf_op jit(solution)/shard_map/ppermute | solution.py:526
  9.5 1.5 %collective-permute-start.4 = (f32[32,128]{1,0:T(8,128)S(1)}, f32[32,128]{1,0:T(8,128)S(1)}, u32[]{:S(2)}, u32[]{:S(2)}) collective-permute-start(f32[32,128]{1,0:T(8,128)S(1)} %get-tuple-element.25), channel_id=1, source_target_pairs={{0,16},{1,17},{2,18},{3,19},{4,20},{5,21},{6,22},{7,23},{8,24},{9,... | collective-permute-start | bytes 49160 | tf_op jit(solution)/shard_map/ppermute | solution.py:526
  11.1 2.6 %collective-permute-start.3 = (f32[32,128]{1,0:T(8,128)S(1)}, f32[32,128]{1,0:T(8,128)S(1)}, u32[]{:S(2)}, u32[]{:S(2)}) collective-permute-start(f32[32,128]{1,0:T(8,128)S(1)} %get-tuple-element.25), channel_id=1, source_target_pairs={{0,2},{1,3},{2,0},{3,1},{4,6},{5,7},{6,4},{7,5},{8,10},{9,11},{10,... | collective-permute-start | bytes 49160 | tf_op jit(solution)/shard_map/ppermute | solution.py:526
  13.6 0.0 collective-permute-done.4.refs_8_
  13.6 2.1 %collective-permute-done.3.refs_7_ = f32[32,128]{1,0:T(8,128)S(1)} collective-permute-done((f32[32,128]{1,0:T(8,128)S(1)}, f32[32,128]{1,0:T(8,128)S(1)}, u32[]{:S(2)}, u32[]{:S(2)}) %collective-permute-start.3) | collective-permute-done | bytes 16416 | tf_op jit(solution)/shard_map/ppermute | solution.py:526
  15.8 0.0 collective-permute-done.refs_4_.refs_6_
  15.8 0.0 collective-permute-done.1.refs_5_.refs_7_
  15.8 0.0 copy-start.4
  15.8 0.0 copy-start.6
  15.8 0.7 %copy-done.4 = s32[27,3,1]{0,2,1:T(1,128)S(1)} copy-done((s32[27,3,1]{0,2,1:T(1,128)S(1)}, s32[27,3,1]{0,2,1:T(1,128)}, u32[]{:S(2)}) %copy-start.4) | copy-done | bytes 348
  16.4 0.0 copy-done.6
  16.5 8.0 %second.1 = (f32[3,32,128]{2,1,0:T(8,128)S(1)}, f32[1,128]{1,0:T(1,128)S(1)}, f32[32,128]{1,0:T(8,128)S(1)}, f32[64,128]{1,0:T(8,128)S(1)}, f32[64,128]{1,0:T(8,128)S(1)}, /*index=5*/f32[64,128]{1,0:T(8,128)S(1)}) custom-call(s32[2,27]{1,0:T(2,128)S(1)} %bitcast.13, s32[3,1,27]{2,1,0:T(1,128)S(1)} %bitcast.10, ...), custom_call_target="tpu_custom_call" | custom-call | tf_op jit(solution)/shard_map/second/pallas_call | solution.py:583
  24.5 0.5 collective-permute-start.5
  25.0 2.6 %collective-permute-start.6 = (f32[33,128]{1,0:T(8,128)S(1)}, f32[33,128]{1,0:T(8,128)S(1)}, u32[]{:S(2)}, u32[]{:S(2)}) collective-permute-start(f32[33,128]{1,0:T(8,128)S(1)} %pad_maximum_fusion.4), channel_id=1, source_target_pairs={{0,2},{1,3},{2,0},{3,1},{4,6},{5,7},{6,4},{7,5},{8,10},{9,11},{10,... | collective-permute-start | bytes 50696 | tf_op jit(solution)/shard_map/ppermute | solution.py:526
  27.6 1.4 %collective-permute-start.7 = (f32[1,128]{1,0:T(1,128)S(1)}, f32[1,128]{1,0:T(1,128)S(1)}, u32[]{:S(2)}, u32[]{:S(2)}) collective-permute-start(f32[1,128]{1,0:T(1,128)S(1)} %get-tuple-element.27), channel_id=1, source_target_pairs={{0,3},{1,2},{2,1},{3,0},{4,7},{5,6},{6,5},{7,4},{8,11},{9,10},{10,... | collective-permute-start | bytes 1544 | tf_op jit(solution)/shard_map/ppermute | solution.py:526
  29.0 4.0 %collective-permute-done.7 = f32[1,128]{1,0:T(1,128)S(1)} collective-permute-done((f32[1,128]{1,0:T(1,128)S(1)}, f32[1,128]{1,0:T(1,128)S(1)}, u32[]{:S(2)}, u32[]{:S(2)}) %collective-permute-start.7) | collective-permute-done | bytes 544 | tf_op jit(solution)/shard_map/ppermute | solution.py:526
  33.0 0.6 %collective-permute-start.8 = (f32[65,128]{1,0:T(8,128)S(1)}, f32[65,128]{1,0:T(8,128)S(1)}, u32[]{:S(2)}, u32[]{:S(2)}) collective-permute-start(f32[65,128]{1,0:T(8,128)S(1)} %pad_maximum_fusion.1), channel_id=1, source_target_pairs={{0,4},{1,5},{2,6},{3,7},{4,0},{5,1},{6,2},{7,3},{8,12},{9,13},{10,... | collective-permute-start | bytes 99848 | tf_op jit(solution)/shard_map/ppermute | solution.py:526
  33.6 3.4 %collective-permute-done.8.refs_10_ = f32[65,128]{1,0:T(8,128)S(1)} collective-permute-done((f32[65,128]{1,0:T(8,128)S(1)}, f32[65,128]{1,0:T(8,128)S(1)}, u32[]{:S(2)}, u32[]{:S(2)}) %collective-permute-start.8) | collective-permute-done | bytes 33312 | tf_op jit(solution)/shard_map/ppermute | solution.py:526
  37.0 0.1 collective-permute-start.9
  37.1 0.6 collective-permute-start.10
  37.7 1.3 %collective-permute-start.11 = (f32[1,128]{1,0:T(1,128)S(1)}, f32[1,128]{1,0:T(1,128)S(1)}, u32[]{:S(2)}, u32[]{:S(2)}) collective-permute-start(f32[1,128]{1,0:T(1,128)S(1)} %slice_maximum_fusion.2), channel_id=1, source_target_pairs={{0,24},{1,25},{2,26},{3,27},{4,28},{5,29},{6,30},{7,31},{8,16},{9,... | collective-permute-start | bytes 1544 | tf_op jit(solution)/shard_map/ppermute | solution.py:526
  39.0 2.0 %collective-permute-done.10 = f32[33,128]{1,0:T(8,128)S(1)} collective-permute-done((f32[33,128]{1,0:T(8,128)S(1)}, f32[33,128]{1,0:T(8,128)S(1)}, u32[]{:S(2)}, u32[]{:S(2)}) %collective-permute-start.10) | collective-permute-done | bytes 16928 | tf_op jit(solution)/shard_map/ppermute | solution.py:526
  41.0 8.1 %third.1 = (f32[3,32,128]{2,1,0:T(8,128)S(1)}, f32[3,32,128]{2,1,0:T(8,128)S(1)}, f32[1,128]{1,0:T(1,128)S(1)}, f32[1,128]{1,0:T(1,128)S(1)}) custom-call(s32[2,27]{1,0:T(2,128)S(1)} %bitcast.14, s32[3,1,27]{2,1,0:T(1,128)S(1)} %bitcast.11, f32[8,32,128]{2,1,0:T(8,128)S(1)} %get-tuple-element.20.refs_2_.base_ref, s32[32,128]{1,0:T(8,128)S(1)} %get-tuple-element.21.refs_3_, ...), custom_call_target="tpu_custom_call" | custom-call | tf_op jit(solution)/shard_map/third/pallas_call | solution.py:610
  49.1 9.4 %all_to_all.5 = f32[32,1,128]{2,1,0:T(1,128)S(1)} all-to-all(f32[32,1,128]{2,1,0:T(1,128)S(1)} %broadcast_in_dim.9), channel_id=1, replica_groups=mesh['gx'=4,'gy'=2,'gz'=4] {'gx','gy','gz'}, dimensions={0} | all-to-all | bytes 32768 | tf_op jit(solution)/shard_map/all_to_all | solution.py:621
  58.5 0.9 %last.1 = (f32[3,3456]{1,0:T(4,128)}, f32[3,3456]{1,0:T(4,128)}, f32[3,3456]{1,0:T(4,128)}, f32[2]{0:T(128)}) custom-call(f32[32,128]{1,0:T(8,128)S(1)} %bitcast.7, f32[8,32,128]{2,1,0:T(8,128)S(1)} %get-tuple-element.20.refs_2_.base_ref, f32[3,32,128]{2,1,0:T(8,128)S(1)} %get-tuple-element.33.pos_ref, ...), custom_call_target="tpu_custom_call" | custom-call | tf_op jit(solution)/shard_map/last/pallas_call | solution.py:622
  (22 shorter events, 0.1 us)
Async XLA Ops:
  0.6 0.7 %copy-start.5 = (s32[27,5,2]{0,2,1:T(2,128)S(1)}, s32[27,5,2]{0,2,1:T(2,128)}, u32[]{:S(2)}) copy-start(s32[27,5,2]{0,2,1:T(2,128)} %param.13) | copy-start | bytes 3244
  1.3 0.8 %copy-start = (f32[3,3456]{1,0:T(4,128)S(1)}, f32[3,3456]{1,0:T(4,128)}, u32[]{:S(2)}) copy-start(f32[3,3456]{1,0:T(4,128)} %refs_0_.1) | copy-start | bytes 124420
  2.1 0.8 %copy-start.1 = (f32[3,3456]{1,0:T(4,128)S(1)}, f32[3,3456]{1,0:T(4,128)}, u32[]{:S(2)}) copy-start(f32[3,3456]{1,0:T(4,128)} %refs_1_.1) | copy-start | bytes 124420
  3.0 0.7 %copy-start.2 = (f32[3456]{0:T(1024)S(1)}, f32[3456]{0:T(1024)}, u32[]{:S(2)}) copy-start(f32[3456]{0:T(1024)} %param.9) | copy-start | bytes 41476
  3.7 0.7 %copy-start.3 = (s32[3456]{0:T(1024)S(1)}, s32[3456]{0:T(1024)}, u32[]{:S(2)}) copy-start(s32[3456]{0:T(1024)} %param.10) | copy-start | bytes 41476
  4.9 10.8 %collective-permute-start = (f32[112,128]{1,0:T(8,128)S(1)}, f32[112,128]{1,0:T(8,128)S(1)}, u32[]{:S(2)}, u32[]{:S(2)}) collective-permute-start(f32[112,128]{1,0:T(8,128)S(1)} %get-tuple-element.22), channel_id=1, source_target_pairs={{0,1},{1,0},{2,3},{3,2},{4,5},{5,4},{6,7},{7,6},{8,9},{9,8},{10,11... | collective-permute-start | bytes 172040 | tf_op jit(solution)/shard_map/ppermute | solution.py:526
  8.0 7.7 %collective-permute-start.1 = (f32[112,128]{1,0:T(8,128)S(1)}, f32[112,128]{1,0:T(8,128)S(1)}, u32[]{:S(2)}, u32[]{:S(2)}) collective-permute-start(f32[112,128]{1,0:T(8,128)S(1)} %get-tuple-element.23), channel_id=1, source_target_pairs={{0,4},{1,5},{2,6},{3,7},{4,0},{5,1},{6,2},{7,3},{8,12},{9,13},{10,... | collective-permute-start | bytes 172040 | tf_op jit(solution)/shard_map/ppermute | solution.py:526
  9.5 6.2 %collective-permute-start.2 = (f32[112,128]{1,0:T(8,128)S(1)}, f32[112,128]{1,0:T(8,128)S(1)}, u32[]{:S(2)}, u32[]{:S(2)}) collective-permute-start(f32[112,128]{1,0:T(8,128)S(1)} %get-tuple-element.24), channel_id=1, source_target_pairs={{0,8},{1,9},{2,10},{3,11},{4,12},{5,13},{6,14},{7,15},{8,0},{9,1},... | collective-permute-start | bytes 172040 | tf_op jit(solution)/shard_map/ppermute | solution.py:526
  9.5 4.1 %collective-permute-start.4 = (f32[32,128]{1,0:T(8,128)S(1)}, f32[32,128]{1,0:T(8,128)S(1)}, u32[]{:S(2)}, u32[]{:S(2)}) collective-permute-start(f32[32,128]{1,0:T(8,128)S(1)} %get-tuple-element.25), channel_id=1, source_target_pairs={{0,16},{1,17},{2,18},{3,19},{4,20},{5,21},{6,22},{7,23},{8,24},{9,... | collective-permute-start | bytes 49160 | tf_op jit(solution)/shard_map/ppermute | solution.py:526
  11.1 4.7 %collective-permute-start.3 = (f32[32,128]{1,0:T(8,128)S(1)}, f32[32,128]{1,0:T(8,128)S(1)}, u32[]{:S(2)}, u32[]{:S(2)}) collective-permute-start(f32[32,128]{1,0:T(8,128)S(1)} %get-tuple-element.25), channel_id=1, source_target_pairs={{0,2},{1,3},{2,0},{3,1},{4,6},{5,7},{6,4},{7,5},{8,10},{9,11},{10,... | collective-permute-start | bytes 49160 | tf_op jit(solution)/shard_map/ppermute | solution.py:526
  15.8 0.7 %copy-start.4 = (s32[27,3,1]{0,2,1:T(1,128)S(1)}, s32[27,3,1]{0,2,1:T(1,128)}, u32[]{:S(2)}) copy-start(s32[27,3,1]{0,2,1:T(1,128)} %param.12) | copy-start | bytes 976
  15.8 0.7 %copy-start.6 = (s32[27,2]{0,1:T(2,128)S(1)}, s32[27,2]{0,1:T(2,128)}, u32[]{:S(2)}) copy-start(s32[27,2]{0,1:T(2,128)} %param.11) | copy-start | bytes 652
  24.5 8.4 %collective-permute-start.5 = (f32[65,128]{1,0:T(8,128)S(1)}, f32[65,128]{1,0:T(8,128)S(1)}, u32[]{:S(2)}, u32[]{:S(2)}) collective-permute-start(f32[65,128]{1,0:T(8,128)S(1)} %pad_maximum_fusion), channel_id=1, source_target_pairs={{0,1},{1,0},{2,3},{3,2},{4,5},{5,4},{6,7},{7,6},{8,9},{9,8},{10,11... | collective-permute-start | bytes 99848 | tf_op jit(solution)/shard_map/ppermute | solution.py:526
  25.0 8.0 %collective-permute-start.6 = (f32[33,128]{1,0:T(8,128)S(1)}, f32[33,128]{1,0:T(8,128)S(1)}, u32[]{:S(2)}, u32[]{:S(2)}) collective-permute-start(f32[33,128]{1,0:T(8,128)S(1)} %pad_maximum_fusion.4), channel_id=1, source_target_pairs={{0,2},{1,3},{2,0},{3,1},{4,6},{5,7},{6,4},{7,5},{8,10},{9,11},{10,... | collective-permute-start | bytes 50696 | tf_op jit(solution)/shard_map/ppermute | solution.py:526
  27.6 5.4 %collective-permute-start.7 = (f32[1,128]{1,0:T(1,128)S(1)}, f32[1,128]{1,0:T(1,128)S(1)}, u32[]{:S(2)}, u32[]{:S(2)}) collective-permute-start(f32[1,128]{1,0:T(1,128)S(1)} %get-tuple-element.27), channel_id=1, source_target_pairs={{0,3},{1,2},{2,1},{3,0},{4,7},{5,6},{6,5},{7,4},{8,11},{9,10},{10,... | collective-permute-start | bytes 1544 | tf_op jit(solution)/shard_map/ppermute | solution.py:526
  33.0 4.0 %collective-permute-start.8 = (f32[65,128]{1,0:T(8,128)S(1)}, f32[65,128]{1,0:T(8,128)S(1)}, u32[]{:S(2)}, u32[]{:S(2)}) collective-permute-start(f32[65,128]{1,0:T(8,128)S(1)} %pad_maximum_fusion.1), channel_id=1, source_target_pairs={{0,4},{1,5},{2,6},{3,7},{4,0},{5,1},{6,2},{7,3},{8,12},{9,13},{10,... | collective-permute-start | bytes 99848 | tf_op jit(solution)/shard_map/ppermute | solution.py:526
  37.0 3.9 %collective-permute-start.9 = (f32[65,128]{1,0:T(8,128)S(1)}, f32[65,128]{1,0:T(8,128)S(1)}, u32[]{:S(2)}, u32[]{:S(2)}) collective-permute-start(f32[65,128]{1,0:T(8,128)S(1)} %pad_maximum_fusion.2), channel_id=1, source_target_pairs={{0,8},{1,9},{2,10},{3,11},{4,12},{5,13},{6,14},{7,15},{8,0},{9,1},... | collective-permute-start | bytes 99848 | tf_op jit(solution)/shard_map/ppermute | solution.py:526
  37.1 3.8 %collective-permute-start.10 = (f32[33,128]{1,0:T(8,128)S(1)}, f32[33,128]{1,0:T(8,128)S(1)}, u32[]{:S(2)}, u32[]{:S(2)}) collective-permute-start(f32[33,128]{1,0:T(8,128)S(1)} %pad_maximum_fusion.3), channel_id=1, source_target_pairs={{0,16},{1,17},{2,18},{3,19},{4,20},{5,21},{6,22},{7,23},{8,24},{9,... | collective-permute-start | bytes 50696 | tf_op jit(solution)/shard_map/ppermute | solution.py:526
  37.7 3.3 %collective-permute-start.11 = (f32[1,128]{1,0:T(1,128)S(1)}, f32[1,128]{1,0:T(1,128)S(1)}, u32[]{:S(2)}, u32[]{:S(2)}) collective-permute-start(f32[1,128]{1,0:T(1,128)S(1)} %slice_maximum_fusion.2), channel_id=1, source_target_pairs={{0,24},{1,25},{2,26},{3,27},{4,28},{5,29},{6,30},{7,31},{8,16},{9,... | collective-permute-start | bytes 1544 | tf_op jit(solution)/shard_map/ppermute | solution.py:526

commit v3 on v2

--- a/solution.py
+++ b/solution.py
@@ -15,6 +15,7 @@
 F32 = jnp.float32
 BF16 = jnp.bfloat16
 FAST_GROUPS = 6
+UNROLL = 3
 VMEM_BYTES = 16 * 2**20
 STEP = 16
 
@@ -90,23 +91,32 @@
 PAIRS = ((0, 0), (1, 1), (2, 2), (0, 1), (0, 2), (1, 2))
 
 
+def spread_sums(blocks):
+    rows, size = blocks[0].shape
+    tall = blocks[0] if len(blocks) == 1 else jnp.concatenate(blocks, axis=0)
+    high = tall.astype(BF16)
+    rest = (tall - high.astype(F32)).astype(BF16)
+    sums = dot_nn(jnp.concatenate([high, rest], axis=1), jnp.ones((2 * size, size), BF16))
+    return [sums[i * rows : (i + 1) * rows] for i in range(len(blocks))]
+
+
 def moment_table(mass, parts):
     shape = mass.shape
     lane = lax.broadcasted_iota(jnp.int32, shape, 1)
-    total = lane_sum(mass)
+    count = len(parts)
+    total, *firsts = spread_sums([mass] + [mass * part[c] for part in parts for c in range(3)])
     columns = [(0, total)]
     rel = []
     for k, part in enumerate(parts):
         line = []
         for c in range(3):
-            center = lane_sum(mass * part[c]) / total
+            center = firsts[3 * k + c] / total
             columns.append((k * STEP + 1 + c, center))
             line.append(part[c] - center)
         rel.append(line)
     weighted = [[mass * line[c] for c in range(3)] for line in rel]
-    count = len(parts)
+    terms = []
     for k in range(2 * count - 1):
-        second = []
         for a, b in PAIRS:
             term = None
             for i in range(count):
@@ -114,7 +124,10 @@
                 if 0 <= j < count:
                     item = weighted[i][a] * rel[j][b]
                     term = item if term is None else term + item
-            second.append(lane_sum(term))
+            terms.append(term)
+    seconds = spread_sums(terms)
+    for k in range(2 * count - 1):
+        second = seconds[6 * k : 6 * k + 6]
         trace = second[0] + second[1] + second[2]
         for q in range(6):
             value = 3.0 * second[q] - trace if q < 3 else 3.0 * second[q]
@@ -193,18 +206,45 @@
             ref[pl.ds(plan.row_m + s, 1), :] = base_ref[3, pl.ds(row, 1), :]
 
 
-def far_field(plan, far_ref, tables, target):
+def far_picks(plan, far_ref, pick_ref):
     rows, size = plan.rows, plan.size
-    cell = lax.broadcasted_iota(jnp.int32, (rows, rows), 1)
-    far_ids = far_ref[...]
+    lane = lax.broadcasted_iota(jnp.int32, (rows, size), 1)
+    ids = far_ref[...].astype(F32)
+    items = plan.levels * plan.km
+    tall = jnp.concatenate([jnp.where(lane == i, ids, 0.0) for i in range(items)], axis=0)
+    spread = dot_nn(tall.astype(BF16), jnp.ones((size, size), BF16))
+    cell = jnp.where(lane < 3 * rows, lane % rows, -1).astype(F32)
+    for i in range(items):
+        hit = spread[i * rows : (i + 1) * rows] == cell
+        pick_ref[i] = jnp.where(hit, 1.0, 0.0).astype(BF16)
+
+
+def far_field(plan, pick_ref, tables, target):
+    rows, size = plan.rows, plan.size
     total = [jnp.zeros((rows, size), F32) for _ in range(3)]
+    one = jnp.where(
+        lax.broadcasted_iota(jnp.int32, (16, size), 0)
+        == lax.broadcasted_iota(jnp.int32, (16, size), 1),
+        1.0,
+        0.0,
+    ).astype(BF16)
+    half = lax.broadcasted_iota(jnp.int32, (2 * size, 2 * size), 0) < size
+    left = lax.broadcasted_iota(jnp.int32, (2 * size, 2 * size), 1) < size
+    ones = jnp.where(half == left, 1.0, 0.0).astype(BF16)
+    blank = jnp.zeros((size - 3 * rows, size), BF16)
     for level in range(plan.levels):
-        parts = split3(tables[level])
+        flat = dot_nt(one, jnp.concatenate([*split3(tables[level]), blank], axis=0)).astype(BF16)
+        wide = [jnp.broadcast_to(flat[p : p + 1], (rows, size)) for p in range(10)]
+        picks = [pick_ref[level * plan.km + k] for k in range(plan.km)]
+        tall = [
+            jnp.concatenate([pick * wide[p], pick * wide[p + 5]], axis=1)
+            for pick in picks
+            for p in range(5)
+        ]
+        got = dot_nn(jnp.concatenate(tall, axis=0), ones)
         for k in range(plan.km):
-            where = level * plan.km + k
-            pick = jnp.where(far_ids[:, where : where + 1] == cell, 1.0, 0.0).astype(BF16)
-            got = dot_nn(pick, parts[0]) + dot_nn(pick, parts[1]) + dot_nn(pick, parts[2])
-            q = [jnp.broadcast_to(got[:, p : p + 1], (rows, size)) for p in range(10)]
+            own = [got[(5 * k + p) * rows : (5 * k + p + 1) * rows] for p in range(5)]
+            q = [part[:, :size] for part in own] + [part[:, size:] for part in own]
             r = [target[c] - q[1 + c] for c in range(3)]
             inverse = lax.rsqrt(r[0] * r[0] + r[1] * r[1] + r[2] * r[2] + SOFT2)
             inverse_sq = inverse * inverse
@@ -222,43 +262,44 @@
     return total
 
 
-def near_field(plan, list_ref, src_ref, face_ref, rank_ref, row_ref, comp_ref, part_ref):
-    tiles, size = plan.tiles, plan.size
-    kl, kn = plan.kl, plan.kn
-    per_tile = kl + 3 * kn
-    fast = FAST_GROUPS * 8
-    last = tiles - 1
-
-    def one_hot(t, first, count):
-        slot = lax.broadcasted_iota(jnp.int32, (count, size), 0).astype(F32) + first
-        return rank_ref[pl.ds(t, 1), :] == slot
-
-    def compact(t, first, count):
-        pick = jnp.where(one_hot(t, first, count), 1.0, 0.0).astype(BF16)
+class Near:
+    def __init__(self, plan, rank_ref, src_ref, lists, face_ref=None):
+        self.plan = plan
+        self.rank_ref = rank_ref
+        self.src_ref = src_ref
+        self.lists = lists
+        self.face_ref = face_ref
+
+    def one_hot(self, t, first, count):
+        slot = lax.broadcasted_iota(jnp.int32, (count, self.plan.size), 0).astype(F32)
+        return self.rank_ref[pl.ds(t, 1), :] == slot + first
+
+    def compact(self, t, first, count, values):
+        size = self.plan.size
+        pick = jnp.where(self.one_hot(t, first, count), 1.0, 0.0).astype(BF16)
         sub = lax.broadcasted_iota(jnp.int32, (8, size), 0)
-        own = jnp.where(
-            sub == 0,
-            src_ref[0, pl.ds(t, 1), :],
-            jnp.where(sub == 1, src_ref[1, pl.ds(t, 1), :], src_ref[2, pl.ds(t, 1), :]),
-        )
+        own = jnp.broadcast_to(values[-1], (8, size))
+        for i in range(len(values) - 2, -1, -1):
+            own = jnp.where(sub == i, values[i], own)
         high, middle, low = split3(own)
         return dot_nt(pick, high) + dot_nt(pick, middle) + dot_nt(pick, low)
 
-    def source_rows(t):
+    def local_rows(self, t):
         found = []
-        for s in range(per_tile):
-            if s < kl:
-                index = list_ref[0][s, t]
-                found.append([src_ref[c, pl.ds(index, 1), :] for c in range(4)])
-            else:
-                slot = (s - kl) // kn
-                index = list_ref[1][slot, (s - kl) % kn, t]
-                found.append([face_ref[slot, c, pl.ds(index, 1), :] for c in range(4)])
+        for s in range(self.plan.kl):
+            index = self.lists[0][s, t]
+            found.append([self.src_ref[c, pl.ds(index, 1), :] for c in range(4)])
         return found
 
-    def pair_sums(packed, sources):
-        here = [jnp.broadcast_to(packed[:, c : c + 1], (8, size)) for c in range(3)]
-        sums = None
+    def remote_rows(self, t):
+        found = []
+        for slot in range(3):
+            for k in range(self.plan.kn):
+                index = self.lists[1][slot, k, t]
+                found.append([self.face_ref[slot, c, pl.ds(index, 1), :] for c in range(4)])
+        return found
+
+    def pair_sums(self, here, sources, sums=None):
         for source in sources:
             r = [source[c] - here[c] for c in range(3)]
             inverse = lax.rsqrt(r[0] * r[0] + r[1] * r[1] + r[2] * r[2] + SOFT2)
@@ -267,54 +308,53 @@
             sums = new if sums is None else [sums[c] + new[c] for c in range(3)]
         return sums
 
-    def scatter(t):
+    def spread(self, packed):
+        return [jnp.broadcast_to(packed[:, c : c + 1], (8, self.plan.size)) for c in range(3)]
+
+    def prepare(self, t, comp_ref, wide_ref):
+        shape = (FAST_GROUPS * 8, self.plan.size)
+        for c in range(3):
+            value = jnp.broadcast_to(comp_ref[t, :, pl.ds(c, 1)], shape)
+            for g in range(FAST_GROUPS):
+                wide_ref[t, g, c] = value[g * 8 : g * 8 + 8]
+
+    def force(self, t, rows, wide_ref, part_ref, init_ref=None):
+        for g in range(FAST_GROUPS):
+            here = [wide_ref[t, g, c] for c in range(3)]
+            sums = None if init_ref is None else [init_ref[t, g, c] for c in range(3)]
+            for c, value in enumerate(self.pair_sums(here, rows, sums)):
+                part_ref[t, g, c] = value
+
+    def scatter(self, t, part_ref, row_ref):
         out = [None] * 3
         for g in range(FAST_GROUPS):
-            mask = one_hot(t, g * 8, 8)
+            mask = self.one_hot(t, g * 8, 8)
             for c in range(3):
-                column = lane_sum(part_ref[t, g, c])
-                value = jnp.where(mask, column, 0.0)
+                value = jnp.where(mask, lane_sum(part_ref[t, g, c]), 0.0)
                 out[c] = value if out[c] is None else out[c] + value
         for c in range(3):
             row_ref[c, pl.ds(t, 1), :] = jnp.sum(out[c], axis=0, keepdims=True)
 
-    def force(t):
-        sources = source_rows(t)
-        for g in range(FAST_GROUPS):
-            sums = pair_sums(comp_ref[t, pl.ds(g * 8, 8), :], sources)
-            for c in range(3):
-                part_ref[t, g, c] = sums[c]
-
-    comp_ref[0, :, pl.ds(0, 8)] = compact(0, 0, fast)
-
-    def body(t, carry):
-        scatter(jnp.maximum(t - 1, 0))
-        force(t)
-        after = jnp.minimum(t + 1, last)
-        comp_ref[after, :, pl.ds(0, 8)] = compact(after, 0, fast)
-        return carry
-
-    lax.fori_loop(0, tiles, body, 0)
-    scatter(last)
-
-    @pl.when(jnp.max(rank_ref[...]) >= fast)
-    def _():
-        def tile_rest(t, carry):
-            def group(g, inner):
-                packed = compact(t, g * 8, 8)
-                sums = pair_sums(packed, source_rows(t))
-                mask = one_hot(t, g * 8, 8)
-                for c in range(3):
-                    value = jnp.where(mask, lane_sum(sums[c]), 0.0)
-                    old = row_ref[c, pl.ds(t, 1), :]
-                    row_ref[c, pl.ds(t, 1), :] = old + jnp.sum(value, axis=0, keepdims=True)
-                return inner
-
-            groups = (jnp.max(rank_ref[pl.ds(t, 1), :]).astype(jnp.int32) + 8) // 8
-            lax.fori_loop(FAST_GROUPS, groups, group, 0)
-            return carry
-
-        lax.fori_loop(0, tiles, tile_rest, 0)
+    def rest(self, row_ref):
+        @pl.when(jnp.max(self.rank_ref[...]) >= FAST_GROUPS * 8)
+        def _():
+            def tile_rest(t, carry):
+                def group(g, inner):
+                    values = [self.src_ref[c, pl.ds(t, 1), :] for c in range(3)]
+                    here = self.spread(self.compact(t, g * 8, 8, values))
+                    sums = self.pair_sums(here, self.local_rows(t) + self.remote_rows(t))
+                    mask = self.one_hot(t, g * 8, 8)
+                    for c in range(3):
+                        value = jnp.where(mask, lane_sum(sums[c]), 0.0)
+                        old = row_ref[c, pl.ds(t, 1), :]
+                        row_ref[c, pl.ds(t, 1), :] = old + jnp.sum(value, axis=0, keepdims=True)
+                    return inner
+
+                most = jnp.max(self.rank_ref[pl.ds(t, 1), :]).astype(jnp.int32)
+                lax.fori_loop(FAST_GROUPS, (most + 8) // 8, group, 0)
+                return carry
+
+            lax.fori_loop(0, self.plan.tiles, tile_rest, 0)
 
 
 def shift_of(plan, level, bit):
@@ -323,8 +363,7 @@
     return jnp.where(bit == 0, span, -span).astype(F32)
 
 
-def lists_start(ins, scratch):
-    outs, sems = scratch[:2], scratch[2]
+def lists_start(ins, outs, sems):
     copies = [pltpu.make_async_copy(ins[i], outs[i], sems.at[i]) for i in range(2)]
     for copy in copies:
         copy.start()
@@ -337,18 +376,54 @@
     return arrived
 
 
-def forces(plan, act, target, tables, arrived, far_ref, src_ref, face_ref, scratch):
-    rank_ref, row_ref, comp_ref, part_ref = scratch
-    rows, size = plan.rows, plan.size
+def rank_rows(plan, act):
+    size = plan.size
     below = lax.broadcasted_iota(jnp.int32, (size, size), 0) < lax.broadcasted_iota(
         jnp.int32, (size, size), 1
     )
     rank = dot_nn(act.astype(BF16), jnp.where(below, 1.0, 0.0).astype(BF16))
-    rank_ref[...] = jnp.where(act > 0, rank, -1.0)
-    row_ref[...] = jnp.zeros(row_ref.shape, F32)
-    far = far_field(plan, far_ref, tables, target)
-    near_field(plan, arrived(), src_ref, face_ref, rank_ref, row_ref, comp_ref, part_ref)
-    return [act * (GRAV * (row_ref[c] + far[c])) for c in range(3)]
+    return jnp.where(act > 0, rank, -1.0)
+
+
+def tile_loop(plan, step):
+    def body(i, carry):
+        step([jnp.minimum(i * UNROLL + j, plan.tiles - 1) for j in range(UNROLL)])
+        return carry
+
+    lax.fori_loop(0, (plan.tiles + UNROLL - 1) // UNROLL, body, 0)
+
+
+def local_kernel(plan, *refs):
+    arrived = lists_start(refs[:2], refs[-3:-1], refs[-1])
+    base_ref, far_ref, rank_ref, pick_ref, comp_ref, wide_ref, part_ref = refs[2:9]
+    tiles = plan.tiles
+    rank_ref[...] = rank_rows(plan, base_ref[7])
+    far_picks(plan, far_ref, pick_ref)
+    near = Near(plan, rank_ref, base_ref, None)
+    for t in range(tiles):
+        own = base_ref[7, pl.ds(t, 1), :]
+        values = [base_ref[c, pl.ds(t, 1), :] for c in range(3)]
+        values += [base_ref[4 + c, pl.ds(t, 1), :] * own for c in range(3)]
+        comp_ref[t, :, pl.ds(0, 8)] = near.compact(t, 0, FAST_GROUPS * 8, values)
+    for j in range(UNROLL):
+        near.prepare(min(j, tiles - 1), comp_ref, wide_ref)
+    near.lists = arrived()
+
+    def step(ts):
+        for t in ts:
+            near.force(t, near.local_rows(t), wide_ref, part_ref)
+        for t in ts:
+            near.prepare(jnp.minimum(t + UNROLL, tiles - 1), comp_ref, wide_ref)
+
+    tile_loop(plan, step)
+
+
+def gather_kernel(plan, rank_ref, comp_ref, acc_ref, u_ref, a_ref):
+    near = Near(plan, rank_ref, acc_ref, None)
+    for t in range(plan.tiles):
+        values = [acc_ref[c, pl.ds(t, 1), :] for c in range(3)]
+        a_ref[t, :, pl.ds(0, 8)] = near.compact(t, 0, FAST_GROUPS * 8, values)
+        u_ref[t] = pltpu.roll(comp_ref[t], plan.size - 3, 1)
 
 
 def lane_row(plan, level, bit):
@@ -367,23 +442,16 @@
 
 
 def second_kernel(plan, *refs):
-    arrived, refs = lists_start(refs[:2], refs[-10:-7]), refs[2:]
-    base_ref, far_ref = refs[:2]
-    near_refs = refs[2:5]
+    face_ref, part_ref, row_ref, *smem = refs[-6:]
+    arrived, refs = lists_start(refs[:2], smem[:2], smem[2]), refs[2:]
+    base_ref, pick_ref, rank_ref, wide_ref, init_ref = refs[:5]
+    near_refs = refs[5:8]
     extra = plan.levels - 3
-    moment_refs = refs[5 : 5 + extra]
-    acc_ref, max_ref, mom_ref = refs[5 + extra : 8 + extra]
-    send_refs = refs[8 + extra : 11 + extra]
-    src_ref, face_ref, _, *scratch = refs[-7:]
-    rows = plan.rows
+    moment_refs = refs[8 : 8 + extra]
+    acc_ref, max_ref, mom_ref = refs[8 + extra : 11 + extra]
+    send_refs = refs[11 + extra : 14 + extra]
+    rows, tiles = plan.rows, plan.tiles
     bits = device_bits(plan.levels)
-    src_ref[...] = base_ref[pl.ds(0, 4)]
-    tables = []
-    others = list(moment_refs)
-    for level in range(plan.levels):
-        slot = plan.place[level][2]
-        table = near_refs[slot][pl.ds(plan.row_t, rows), :] if slot >= 0 else others.pop(0)[...]
-        tables.append(table + lane_row(plan, level, bits[level]))
     face = plan.face
     for slot in range(3):
         level = plan.near_level[slot]
@@ -394,9 +462,29 @@
                 value = value + shift_of(plan, level, bits[level])
             face_ref[slot, c, pl.ds(0, face), :] = value
         face_ref[slot, 3, pl.ds(0, face), :] = near_refs[slot][pl.ds(plan.row_m, face), :]
+    tables = []
+    others = list(moment_refs)
+    for level in range(plan.levels):
+        slot = plan.place[level][2]
+        table = near_refs[slot][pl.ds(plan.row_t, rows), :] if slot >= 0 else others.pop(0)[...]
+        tables.append(table + lane_row(plan, level, bits[level]))
     act = base_ref[7]
     position = [base_ref[c] for c in range(3)]
-    acc = forces(plan, act, position, tables, arrived, far_ref, src_ref, face_ref, scratch)
+    far = far_field(plan, pick_ref, tables, position)
+    row_ref[...] = jnp.zeros(row_ref.shape, F32)
+    near = Near(plan, rank_ref, base_ref, arrived(), face_ref)
+
+    def step(ts):
+        for t in ts:
+            near.scatter(jnp.maximum(t - UNROLL, 0), part_ref, row_ref)
+        for t in ts:
+            near.force(t, near.remote_rows(t), wide_ref, part_ref, init_ref)
+
+    tile_loop(plan, step)
+    for j in range(UNROLL):
+        near.scatter(max(tiles - 1 - j, 0), part_ref, row_ref)
+    near.rest(row_ref)
+    acc = [act * (GRAV * (row_ref[c] + far[c])) for c in range(3)]
     for c in range(3):
         acc_ref[c] = acc[c]
     max_ref[...] = square_row(acc)
@@ -410,19 +498,18 @@
 
 
 def third_kernel(plan, *refs):
-    arrived, refs = lists_start(refs[:2], refs[-10:-7]), refs[2:]
-    base_ref, far_ref, acc_ref, max_ref = refs[:4]
-    near_refs = refs[4:7]
-    send_refs = refs[7:10]
+    face_ref, part_ref, row_ref, src_ref, moved_ref, slot_ref, wide_ref, *smem = refs[-10:]
+    arrived, refs = lists_start(refs[:2], smem[:2], smem[2]), refs[2:]
+    base_ref, pick_ref, rank_ref, comp_ref, u_ref, a_ref, acc_ref, max_ref = refs[:8]
+    near_refs = refs[8:11]
+    send_refs = refs[11:14]
     extra = plan.levels - 3
-    moment_refs = refs[10 : 10 + extra]
-    pos_ref, out_ref, square_ref, step_ref = refs[10 + extra : 14 + extra]
-    src_ref, face_ref, moved_ref, *scratch = refs[-7:]
-    rows, size = plan.rows, plan.size
+    moment_refs = refs[14 : 14 + extra]
+    pos_ref, out_ref, square_ref, step_ref = refs[14 + extra : 18 + extra]
+    rows, size, tiles = plan.rows, plan.size, plan.tiles
     bits = device_bits(plan.levels)
     step = time_step_of(jnp.max(max_ref[...], axis=(0, 1), keepdims=True))
     step_ref[...] = jnp.broadcast_to(step, step_ref.shape)
-    dt = jnp.broadcast_to(step, (8, size))
     wide = jnp.broadcast_to(step, (rows, size))
     position = []
     act = base_ref[7]
@@ -432,6 +519,9 @@
         src_ref[c] = moved
         position.append(moved)
     src_ref[3] = base_ref[3]
+    slots = jnp.broadcast_to(step, (FAST_GROUPS * 8, size))
+    for t in range(tiles):
+        slot_ref[t] = comp_ref[t] + (u_ref[t] + a_ref[t] * slots) * slots
     lane = lax.broadcasted_iota(jnp.int32, (rows, size), 1)
     tables = []
     others = list(moment_refs)
@@ -449,19 +539,37 @@
     for slot in range(3):
         level = plan.near_level[slot]
         cut = plan.place[level][0]
-        near = near_refs[slot]
-        moved_ref[...] = (
-            near[pl.ds(0, frows), :]
-            + (near[pl.ds(plan.row_u, frows), :] + send_refs[slot][pl.ds(0, frows), :] * fwide)
+        got = near_refs[slot]
+        moved_ref[slot] = (
+            got[pl.ds(0, frows), :]
+            + (got[pl.ds(plan.row_u, frows), :] + send_refs[slot][pl.ds(0, frows), :] * fwide)
             * fwide
         )
         for c in range(3):
-            value = moved_ref[pl.ds(c * face, face), :]
+            value = moved_ref[slot, pl.ds(c * face, face), :]
             if c == cut:
                 value = value + shift_of(plan, level, bits[level])
             face_ref[slot, c, pl.ds(0, face), :] = value
-        face_ref[slot, 3, pl.ds(0, face), :] = near[pl.ds(plan.row_m, face), :]
-    acc = forces(plan, act, position, tables, arrived, far_ref, src_ref, face_ref, scratch)
+        face_ref[slot, 3, pl.ds(0, face), :] = got[pl.ds(plan.row_m, face), :]
+    far = far_field(plan, pick_ref, tables, position)
+    row_ref[...] = jnp.zeros(row_ref.shape, F32)
+    near = Near(plan, rank_ref, src_ref, arrived(), face_ref)
+    for j in range(UNROLL):
+        near.prepare(min(j, tiles - 1), slot_ref, wide_ref)
+
+    def work(ts):
+        for t in ts:
+            near.scatter(jnp.maximum(t - UNROLL, 0), part_ref, row_ref)
+        for t in ts:
+            near.force(t, near.local_rows(t) + near.remote_rows(t), wide_ref, part_ref)
+        for t in ts:
+            near.prepare(jnp.minimum(t + UNROLL, tiles - 1), slot_ref, wide_ref)
+
+    tile_loop(plan, work)
+    for j in range(UNROLL):
+        near.scatter(max(tiles - 1 - j, 0), part_ref, row_ref)
+    near.rest(row_ref)
+    acc = [act * (GRAV * (row_ref[c] + far[c])) for c in range(3)]
     for c in range(3):
         out_ref[c] = acc[c]
     square_ref[...] = square_row(acc)
@@ -495,6 +603,10 @@
 
 def hbm():
     return pl.BlockSpec(memory_space=pltpu.HBM)
+
+
+def in_hbm(values):
+    return pltpu.with_memory_space_constraint(values, pltpu.HBM)
 
 
 def smem():
@@ -549,11 +661,11 @@
         [hbm()] * 5,
         "first",
     )(
-        offsets,
-        velocities,
-        masses.reshape(tiles, size),
-        active.reshape(tiles, size),
-        jnp.transpose(far_list, (1, 2, 0)),
+        in_hbm(offsets),
+        in_hbm(velocities),
+        in_hbm(masses.reshape(tiles, size)),
+        in_hbm(active.reshape(tiles, size)),
+        in_hbm(jnp.transpose(far_list, (1, 2, 0))),
     )
 
     got_near = [None] * 3
@@ -564,29 +676,42 @@
         if plan.place[level][2] < 0:
             got_far.append(exchange(plan, moments, [level]))
 
-    lists = (jnp.transpose(near_local), jnp.transpose(near_remote, (1, 2, 0)))
-    fast = FAST_GROUPS * 8
-    scratch = [
+    lists = (
+        in_hbm(jnp.transpose(near_local)),
+        in_hbm(jnp.transpose(near_remote, (1, 2, 0))),
+    )
+    slots = (tiles, FAST_GROUPS * 8, size)
+    broad = (tiles, FAST_GROUPS, 3, 8, size)
+    list_scratch = [
         pltpu.SMEM((kl, tiles), jnp.int32),
         pltpu.SMEM((3, kn, tiles), jnp.int32),
         pltpu.SemaphoreType.DMA((2,)),
-    ] + buffers(
-        (4, rows, size),
-        (3, 4, up8(plan.face), size),
-        (plan.frows, size),
-        (rows, size),
-        whole,
-        (tiles, fast, size),
-        (tiles, FAST_GROUPS, 3, 8, size),
-    )
+    ]
+    force_scratch = buffers((3, 4, up8(plan.face), size), broad, whole)
+    rank, picks, comp, spread, local = call(
+        functools.partial(local_kernel, plan),
+        floats((rows, size))
+        + [jax.ShapeDtypeStruct((levels * km, rows, size), BF16)]
+        + floats(slots, broad, broad),
+        list_scratch,
+        [hbm(), hbm(), vmem(), vmem()],
+        "local",
+    )(*lists, base, far_ids)
     send_rows = plan.frows + rows
     acc, square, table, *send = call(
         functools.partial(second_kernel, plan),
         floats(whole, (1, size), (rows, size), *[(send_rows, size)] * 3),
-        scratch,
-        [hbm(), hbm()] + [vmem()] * (2 + levels),
+        force_scratch + list_scratch,
+        [hbm(), hbm()] + [vmem()] * (5 + levels),
         "second",
-    )(*lists, base, far_ids, *got_near, *got_far)
+    )(*lists, base, picks, rank, spread, local, *got_near, *got_far)
+    slot_u, slot_a = call(
+        functools.partial(gather_kernel, plan),
+        floats(slots, slots),
+        [],
+        [vmem()] * 3,
+        "gather",
+    )(rank, comp, acc)
 
     got_send = [None] * 3
     got_table = {}
@@ -610,15 +735,17 @@
     moved, acc2, square2, step = call(
         functools.partial(third_kernel, plan),
         floats(whole, whole, (1, size), (1, size)),
-        scratch,
-        [hbm(), hbm()] + [vmem()] * (4 + 3 + 3 + extra),
+        force_scratch
+        + buffers((4, rows, size), (3, plan.frows, size), slots, broad)
+        + list_scratch,
+        [hbm(), hbm()] + [vmem()] * (8 + 3 + 3 + extra),
         "third",
     )(
-        *lists, base, far_ids, acc, best, *got_near, *got_send,
+        *lists, base, picks, rank, comp, slot_u, slot_a, acc, best, *got_near, *got_send,
         *[got_table[level][:rows] for level in range(levels) if plan.place[level][2] < 0],
     )
-    spread = jnp.broadcast_to(square2[None], (plan.devices, 1, size))
-    everyone = lax.all_to_all(spread, AXES, 0, 0).reshape(plan.devices, size)
+    copies = jnp.broadcast_to(square2[None], (plan.devices, 1, size))
+    everyone = lax.all_to_all(copies, AXES, 0, 0).reshape(plan.devices, size)
     pos, vel, out, steps = call(
         functools.partial(last_kernel, plan),
         floats(offsets.shape, offsets.shape, offsets.shape, (SUBSTEPS,)),

time: 59.8 us -> 48.1 us (0.80)
  local copies, waits for them, and re-layouts: 4.44 us -> 0.01 us
  Pallas kernels: 17.6 us -> 13.3 us
  waiting for transfers between devices: 11.5 us -> 8.63 us
    pallas_call x1, Pallas kernels: 8.05 us -> 3.44 us  [body(): call(functools.partial(second_kernel, plan), floats(whole, (1, size), (ro...]
    unnamed x14 -> x0, local copies, waits for them, and re-layouts: 4.42 us -> none
    pallas_call x1, Pallas kernels: 8.13 us -> 4.76 us  [body(): call(functools.partial(third_kernel, plan), floats(whole, whole, (1, size...]
    ppermute x12, waiting for transfers between devices: 11.5 us -> 8.63 us  [exchange(): lax.ppermute(block, AXES, [(i, i ^ flip) for i in range(plan.devices)])]
    pallas_call x0 -> x2, Pallas kernels: none -> 2.84 us  [the longest x1 2.19 us: body(): call(functools.partial(local_kernel, plan), floats((rows, size)) + [jax.S...]
    pallas_call x1, Pallas kernels: 0.53 us -> 1.31 us  [body(): call(functools.partial(first_kernel, plan), floats((8, rows, size), (rows...]
  transfers between devices with their start and end apart: 12 -> 12, of which waited for: 4 -> 3; matrix products, arithmetic and copies ran while one was open for 0% -> 0% of each run, Pallas kernels for 0% -> 6%
where the time goes in v3:
time: 48.1 us; the launch traced here: 47.9 us
  starting transfers between devices  15.7 us (33%)
  Pallas kernels  13.3 us (28%)
  blocking collectives  9.52 us (20%)
  waiting for transfers between devices  8.63 us (18%)
  between operations  0.78 us (2%)
    ppermute x12, starting transfers between devices, exchange(): lax.ppermute(block, AXES, [(i, i ^ flip) for i in range(plan.devices)])  15.7 us
    all_to_all x1, blocking collectives, body(): everyone = lax.all_to_all(copies, AXES, 0, 0).reshape(plan.devices, size)  9.52 us
    ppermute x12, waiting for transfers between devices, exchange(): lax.ppermute(block, AXES, [(i, i ^ flip) for i in range(plan.devices)])  8.63 us
    pallas_call x1, Pallas kernels, body(): call(functools.partial(third_kernel, plan), floats(whole, whole, (1, size...  4.76 us
    pallas_call x1, Pallas kernels, body(): call(functools.partial(second_kernel, plan), floats(whole, (1, size), (ro...  3.44 us
    pallas_call x1, Pallas kernels, body(): call(functools.partial(local_kernel, plan), floats((rows, size)) + [jax.S...  2.19 us
    pallas_call x1, Pallas kernels, body(): call(functools.partial(first_kernel, plan), floats((8, rows, size), (rows...  1.31 us
  transfers between devices with their start and end apart: 12, of which 3 were waited for; matrix products, arithmetic and copies ran while one was open for 0% of the time, Pallas kernels for 6%

profile of v3, /device:TPU:0, one launch (start us, length us, event | category | flops | bytes accessed | tf_op | source)
XLA Modules:
  0.0 47.9 jit_solution(15566809503041265811)
XLA Ops:
  0.6 1.3 %first.1 = (f32[8,32,128]{2,1,0:T(8,128)S(1)}, f32[32,128]{1,0:T(8,128)S(1)}, s32[32,128]{1,0:T(8,128)S(1)}, f32[112,128]{1,0:T(8,128)S(1)}, f32[112,128]{1,0:T(8,128)S(1)}, /*index=5*/f32[112,128]{1,0:T(8,128)S(1)}) custom-call(f32[3,3456]{1,0:T(4,128)} %refs_0_.1, f32[3,3456]{1,0:T(4,128)} %refs_1_.1, f32[27,128]{1,0:T(8,128)} %bitcast.9, ...), custom_call_target="tpu_custom_call" | custom-call | tf_op jit(solution)/shard_map/first/pallas_call | solution.py:650
  2.0 3.1 %collective-permute-start = (f32[112,128]{1,0:T(8,128)S(1)}, f32[112,128]{1,0:T(8,128)S(1)}, u32[]{:S(2)}, u32[]{:S(2)}) collective-permute-start(f32[112,128]{1,0:T(8,128)S(1)} %get-tuple-element.34), channel_id=1, source_target_pairs={{0,1},{1,0},{2,3},{3,2},{4,5},{5,4},{6,7},{7,6},{8,9},{9,8},{10,11... | collective-permute-start | bytes 172040 | tf_op jit(solution)/shard_map/ppermute | solution.py:638
  5.1 1.5 %collective-permute-start.1 = (f32[112,128]{1,0:T(8,128)S(1)}, f32[112,128]{1,0:T(8,128)S(1)}, u32[]{:S(2)}, u32[]{:S(2)}) collective-permute-start(f32[112,128]{1,0:T(8,128)S(1)} %get-tuple-element.35), channel_id=1, source_target_pairs={{0,4},{1,5},{2,6},{3,7},{4,0},{5,1},{6,2},{7,3},{8,12},{9,13},{10,... | collective-permute-start | bytes 172040 | tf_op jit(solution)/shard_map/ppermute | solution.py:638
  6.6 0.0 collective-permute-start.2
  6.6 1.5 %collective-permute-start.4 = (f32[32,128]{1,0:T(8,128)S(1)}, f32[32,128]{1,0:T(8,128)S(1)}, u32[]{:S(2)}, u32[]{:S(2)}) collective-permute-start(f32[32,128]{1,0:T(8,128)S(1)} %get-tuple-element.37), channel_id=1, source_target_pairs={{0,16},{1,17},{2,18},{3,19},{4,20},{5,21},{6,22},{7,23},{8,24},{9,... | collective-permute-start | bytes 49160 | tf_op jit(solution)/shard_map/ppermute | solution.py:638
  8.1 2.6 %collective-permute-start.3 = (f32[32,128]{1,0:T(8,128)S(1)}, f32[32,128]{1,0:T(8,128)S(1)}, u32[]{:S(2)}, u32[]{:S(2)}) collective-permute-start(f32[32,128]{1,0:T(8,128)S(1)} %get-tuple-element.37), channel_id=1, source_target_pairs={{0,2},{1,3},{2,0},{3,1},{4,6},{5,7},{6,4},{7,5},{8,10},{9,11},{10,... | collective-permute-start | bytes 49160 | tf_op jit(solution)/shard_map/ppermute | solution.py:638
  10.7 2.2 %local.1 = (f32[32,128]{1,0:T(8,128)S(1)}, bf16[10,32,128]{2,1,0:T(8,128)(2,1)S(1)}, f32[27,48,128]{2,1,0:T(8,128)S(1)}, f32[27,6,3,8,128]{4,3,2,1,0:T(8,128)S(1)}, f32[27,6,3,8,128]{4,3,2,1,0:T(8,128)S(1)}) custom-call(s32[2,27]{1,0:T(2,128)} %bitcast.14, s32[3,1,27]{2,1,0:T(1,128)} %bitcast.11, f32[8,32,128]{2,1,0:T(8,128)S(1)} %get-tuple-element.27.refs_2_.base_ref, ...), custom_call_target="tpu_custom_call" | custom-call | tf_op jit(solution)/shard_map/local/pallas_call | solution.py:691
  12.9 0.0 collective-permute-done.4.refs_11_
  12.9 0.0 collective-permute-done.3.refs_10_
  12.9 0.0 collective-permute-done.refs_7_.refs_10_
  12.9 0.0 collective-permute-done.1.refs_8_.refs_11_
  12.9 0.0 collective-permute-done.2.refs_9_.refs_12_
  12.9 3.4 %second.1 = (f32[3,32,128]{2,1,0:T(8,128)S(1)}, f32[1,128]{1,0:T(1,128)S(1)}, f32[32,128]{1,0:T(8,128)S(1)}, f32[64,128]{1,0:T(8,128)S(1)}, f32[64,128]{1,0:T(8,128)S(1)}, /*index=5*/f32[64,128]{1,0:T(8,128)S(1)}) custom-call(s32[2,27]{1,0:T(2,128)} %bitcast.15, s32[3,1,27]{2,1,0:T(1,128)} %bitcast.12, f32[8,32,128]{2,1,0:T(8,128)S(1)} %get-tuple-element.27.refs_2_.base_ref, ...), custom_call_target="tpu_custom_call" | custom-call | tf_op jit(solution)/shard_map/second/pallas_call | solution.py:701
  16.4 0.5 %collective-permute-start.5 = (f32[65,128]{1,0:T(8,128)S(1)}, f32[65,128]{1,0:T(8,128)S(1)}, u32[]{:S(2)}, u32[]{:S(2)}) collective-permute-start(f32[65,128]{1,0:T(8,128)S(1)} %pad_maximum_fusion), channel_id=1, source_target_pairs={{0,1},{1,0},{2,3},{3,2},{4,5},{5,4},{6,7},{7,6},{8,9},{9,8},{10,11... | collective-permute-start | bytes 99848 | tf_op jit(solution)/shard_map/ppermute | solution.py:638
  16.9 2.4 %collective-permute-start.6 = (f32[33,128]{1,0:T(8,128)S(1)}, f32[33,128]{1,0:T(8,128)S(1)}, u32[]{:S(2)}, u32[]{:S(2)}) collective-permute-start(f32[33,128]{1,0:T(8,128)S(1)} %pad_maximum_fusion.4), channel_id=1, source_target_pairs={{0,2},{1,3},{2,0},{3,1},{4,6},{5,7},{6,4},{7,5},{8,10},{9,11},{10,... | collective-permute-start | bytes 50696 | tf_op jit(solution)/shard_map/ppermute | solution.py:638
  19.3 1.5 %collective-permute-start.7 = (f32[1,128]{1,0:T(1,128)S(1)}, f32[1,128]{1,0:T(1,128)S(1)}, u32[]{:S(2)}, u32[]{:S(2)}) collective-permute-start(f32[1,128]{1,0:T(1,128)S(1)} %get-tuple-element.41), channel_id=1, source_target_pairs={{0,3},{1,2},{2,1},{3,0},{4,7},{5,6},{6,5},{7,4},{8,11},{9,10},{10,... | collective-permute-start | bytes 1544 | tf_op jit(solution)/shard_map/ppermute | solution.py:638
  20.9 3.8 %collective-permute-done.7 = f32[1,128]{1,0:T(1,128)S(1)} collective-permute-done((f32[1,128]{1,0:T(1,128)S(1)}, f32[1,128]{1,0:T(1,128)S(1)}, u32[]{:S(2)}, u32[]{:S(2)}) %collective-permute-start.7) | collective-permute-done | bytes 544 | tf_op jit(solution)/shard_map/ppermute | solution.py:638
  24.7 0.0 collective-permute-done.6
  24.7 0.0 collective-permute-done.5.refs_13_
  24.7 0.6 %collective-permute-start.8 = (f32[65,128]{1,0:T(8,128)S(1)}, f32[65,128]{1,0:T(8,128)S(1)}, u32[]{:S(2)}, u32[]{:S(2)}) collective-permute-start(f32[65,128]{1,0:T(8,128)S(1)} %pad_maximum_fusion.1), channel_id=1, source_target_pairs={{0,4},{1,5},{2,6},{3,7},{4,0},{5,1},{6,2},{7,3},{8,12},{9,13},{10,... | collective-permute-start | bytes 99848 | tf_op jit(solution)/shard_map/ppermute | solution.py:638
  25.3 3.4 %collective-permute-done.8.refs_14_ = f32[65,128]{1,0:T(8,128)S(1)} collective-permute-done((f32[65,128]{1,0:T(8,128)S(1)}, f32[65,128]{1,0:T(8,128)S(1)}, u32[]{:S(2)}, u32[]{:S(2)}) %collective-permute-start.8) | collective-permute-done | bytes 33312 | tf_op jit(solution)/shard_map/ppermute | solution.py:638
  28.7 0.1 collective-permute-start.9
  28.8 0.6 %collective-permute-start.10 = (f32[33,128]{1,0:T(8,128)S(1)}, f32[33,128]{1,0:T(8,128)S(1)}, u32[]{:S(2)}, u32[]{:S(2)}) collective-permute-start(f32[33,128]{1,0:T(8,128)S(1)} %pad_maximum_fusion.3), channel_id=1, source_target_pairs={{0,16},{1,17},{2,18},{3,19},{4,20},{5,21},{6,22},{7,23},{8,24},{9,... | collective-permute-start | bytes 50696 | tf_op jit(solution)/shard_map/ppermute | solution.py:638
  29.4 1.3 %collective-permute-start.11 = (f32[1,128]{1,0:T(1,128)S(1)}, f32[1,128]{1,0:T(1,128)S(1)}, u32[]{:S(2)}, u32[]{:S(2)}) collective-permute-start(f32[1,128]{1,0:T(1,128)S(1)} %slice_maximum_fusion.2), channel_id=1, source_target_pairs={{0,24},{1,25},{2,26},{3,27},{4,28},{5,29},{6,30},{7,31},{8,16},{9,... | collective-permute-start | bytes 1544 | tf_op jit(solution)/shard_map/ppermute | solution.py:638
  30.7 0.7 %gather.1 = (f32[27,48,128]{2,1,0:T(8,128)S(1)}, f32[27,48,128]{2,1,0:T(8,128)S(1)}) custom-call(f32[32,128]{1,0:T(8,128)S(1)} %get-tuple-element.30.refs_4_.rank_ref, f32[27,48,128]{2,1,0:T(8,128)S(1)} %get-tuple-element.31.comp_ref.refs_5_, f32[3,32,128]{2,1,0:T(8,128)S(1)} %get-tuple-element.38.acc_ref.refs_8_.first_ref), custom_call_target="tpu_custom_call" | custom-call | tf_op jit(solution)/shard_map/gather/pallas_call | solution.py:708
  31.3 1.3 %collective-permute-done.10 = f32[33,128]{1,0:T(8,128)S(1)} collective-permute-done((f32[33,128]{1,0:T(8,128)S(1)}, f32[33,128]{1,0:T(8,128)S(1)}, u32[]{:S(2)}, u32[]{:S(2)}) %collective-permute-start.10) | collective-permute-done | bytes 16928 | tf_op jit(solution)/shard_map/ppermute | solution.py:638
  32.7 0.0 collective-permute-done.11
  32.7 0.0 collective-permute-done.9.refs_15_
  32.7 4.8 %third.1 = (f32[3,32,128]{2,1,0:T(8,128)S(1)}, f32[3,32,128]{2,1,0:T(8,128)S(1)}, f32[1,128]{1,0:T(1,128)S(1)}, f32[1,128]{1,0:T(1,128)S(1)}) custom-call(s32[2,27]{1,0:T(2,128)} %bitcast.16, s32[3,1,27]{2,1,0:T(1,128)} %bitcast.13, f32[8,32,128]{2,1,0:T(8,128)S(1)} %get-tuple-element.27.refs_2_.base_ref, ...), custom_call_target="tpu_custom_call" | custom-call | tf_op jit(solution)/shard_map/third/pallas_call | solution.py:735
  37.5 9.5 %all_to_all.5 = f32[32,1,128]{2,1,0:T(1,128)S(1)} all-to-all(f32[32,1,128]{2,1,0:T(1,128)S(1)} %broadcast_in_dim.9), channel_id=1, replica_groups=mesh['gx'=4,'gy'=2,'gz'=4] {'gx','gy','gz'}, dimensions={0} | all-to-all | bytes 32768 | tf_op jit(solution)/shard_map/all_to_all | solution.py:748
  47.0 0.9 %last.1 = (f32[3,3456]{1,0:T(4,128)}, f32[3,3456]{1,0:T(4,128)}, f32[3,3456]{1,0:T(4,128)}, f32[2]{0:T(128)}) custom-call(f32[32,128]{1,0:T(8,128)S(1)} %bitcast.7, f32[8,32,128]{2,1,0:T(8,128)S(1)} %get-tuple-element.27.refs_2_.base_ref, f32[3,32,128]{2,1,0:T(8,128)S(1)} %get-tuple-element.47.pos_ref, ...), custom_call_target="tpu_custom_call" | custom-call | tf_op jit(solution)/shard_map/last/pallas_call | solution.py:749
  (11 shorter events, 0.1 us)
Async XLA Ops:
  2.0 10.9 %collective-permute-start = (f32[112,128]{1,0:T(8,128)S(1)}, f32[112,128]{1,0:T(8,128)S(1)}, u32[]{:S(2)}, u32[]{:S(2)}) collective-permute-start(f32[112,128]{1,0:T(8,128)S(1)} %get-tuple-element.34), channel_id=1, source_target_pairs={{0,1},{1,0},{2,3},{3,2},{4,5},{5,4},{6,7},{7,6},{8,9},{9,8},{10,11... | collective-permute-start | bytes 172040 | tf_op jit(solution)/shard_map/ppermute | solution.py:638
  5.1 7.8 %collective-permute-start.1 = (f32[112,128]{1,0:T(8,128)S(1)}, f32[112,128]{1,0:T(8,128)S(1)}, u32[]{:S(2)}, u32[]{:S(2)}) collective-permute-start(f32[112,128]{1,0:T(8,128)S(1)} %get-tuple-element.35), channel_id=1, source_target_pairs={{0,4},{1,5},{2,6},{3,7},{4,0},{5,1},{6,2},{7,3},{8,12},{9,13},{10,... | collective-permute-start | bytes 172040 | tf_op jit(solution)/shard_map/ppermute | solution.py:638
  6.6 6.4 %collective-permute-start.2 = (f32[112,128]{1,0:T(8,128)S(1)}, f32[112,128]{1,0:T(8,128)S(1)}, u32[]{:S(2)}, u32[]{:S(2)}) collective-permute-start(f32[112,128]{1,0:T(8,128)S(1)} %get-tuple-element.36), channel_id=1, source_target_pairs={{0,8},{1,9},{2,10},{3,11},{4,12},{5,13},{6,14},{7,15},{8,0},{9,1},... | collective-permute-start | bytes 172040 | tf_op jit(solution)/shard_map/ppermute | solution.py:638
  6.6 6.3 %collective-permute-start.4 = (f32[32,128]{1,0:T(8,128)S(1)}, f32[32,128]{1,0:T(8,128)S(1)}, u32[]{:S(2)}, u32[]{:S(2)}) collective-permute-start(f32[32,128]{1,0:T(8,128)S(1)} %get-tuple-element.37), channel_id=1, source_target_pairs={{0,16},{1,17},{2,18},{3,19},{4,20},{5,21},{6,22},{7,23},{8,24},{9,... | collective-permute-start | bytes 49160 | tf_op jit(solution)/shard_map/ppermute | solution.py:638
  8.1 4.8 %collective-permute-start.3 = (f32[32,128]{1,0:T(8,128)S(1)}, f32[32,128]{1,0:T(8,128)S(1)}, u32[]{:S(2)}, u32[]{:S(2)}) collective-permute-start(f32[32,128]{1,0:T(8,128)S(1)} %get-tuple-element.37), channel_id=1, source_target_pairs={{0,2},{1,3},{2,0},{3,1},{4,6},{5,7},{6,4},{7,5},{8,10},{9,11},{10,... | collective-permute-start | bytes 49160 | tf_op jit(solution)/shard_map/ppermute | solution.py:638
  16.4 8.3 %collective-permute-start.5 = (f32[65,128]{1,0:T(8,128)S(1)}, f32[65,128]{1,0:T(8,128)S(1)}, u32[]{:S(2)}, u32[]{:S(2)}) collective-permute-start(f32[65,128]{1,0:T(8,128)S(1)} %pad_maximum_fusion), channel_id=1, source_target_pairs={{0,1},{1,0},{2,3},{3,2},{4,5},{5,4},{6,7},{7,6},{8,9},{9,8},{10,11... | collective-permute-start | bytes 99848 | tf_op jit(solution)/shard_map/ppermute | solution.py:638
  16.9 7.8 %collective-permute-start.6 = (f32[33,128]{1,0:T(8,128)S(1)}, f32[33,128]{1,0:T(8,128)S(1)}, u32[]{:S(2)}, u32[]{:S(2)}) collective-permute-start(f32[33,128]{1,0:T(8,128)S(1)} %pad_maximum_fusion.4), channel_id=1, source_target_pairs={{0,2},{1,3},{2,0},{3,1},{4,6},{5,7},{6,4},{7,5},{8,10},{9,11},{10,... | collective-permute-start | bytes 50696 | tf_op jit(solution)/shard_map/ppermute | solution.py:638
  19.3 5.4 %collective-permute-start.7 = (f32[1,128]{1,0:T(1,128)S(1)}, f32[1,128]{1,0:T(1,128)S(1)}, u32[]{:S(2)}, u32[]{:S(2)}) collective-permute-start(f32[1,128]{1,0:T(1,128)S(1)} %get-tuple-element.41), channel_id=1, source_target_pairs={{0,3},{1,2},{2,1},{3,0},{4,7},{5,6},{6,5},{7,4},{8,11},{9,10},{10,... | collective-permute-start | bytes 1544 | tf_op jit(solution)/shard_map/ppermute | solution.py:638
  24.7 4.0 %collective-permute-start.8 = (f32[65,128]{1,0:T(8,128)S(1)}, f32[65,128]{1,0:T(8,128)S(1)}, u32[]{:S(2)}, u32[]{:S(2)}) collective-permute-start(f32[65,128]{1,0:T(8,128)S(1)} %pad_maximum_fusion.1), channel_id=1, source_target_pairs={{0,4},{1,5},{2,6},{3,7},{4,0},{5,1},{6,2},{7,3},{8,12},{9,13},{10,... | collective-permute-start | bytes 99848 | tf_op jit(solution)/shard_map/ppermute | solution.py:638
  28.7 3.9 %collective-permute-start.9 = (f32[65,128]{1,0:T(8,128)S(1)}, f32[65,128]{1,0:T(8,128)S(1)}, u32[]{:S(2)}, u32[]{:S(2)}) collective-permute-start(f32[65,128]{1,0:T(8,128)S(1)} %pad_maximum_fusion.2), channel_id=1, source_target_pairs={{0,8},{1,9},{2,10},{3,11},{4,12},{5,13},{6,14},{7,15},{8,0},{9,1},... | collective-permute-start | bytes 99848 | tf_op jit(solution)/shard_map/ppermute | solution.py:638
  28.8 3.8 %collective-permute-start.10 = (f32[33,128]{1,0:T(8,128)S(1)}, f32[33,128]{1,0:T(8,128)S(1)}, u32[]{:S(2)}, u32[]{:S(2)}) collective-permute-start(f32[33,128]{1,0:T(8,128)S(1)} %pad_maximum_fusion.3), channel_id=1, source_target_pairs={{0,16},{1,17},{2,18},{3,19},{4,20},{5,21},{6,22},{7,23},{8,24},{9,... | collective-permute-start | bytes 50696 | tf_op jit(solution)/shard_map/ppermute | solution.py:638
  29.4 3.3 %collective-permute-start.11 = (f32[1,128]{1,0:T(1,128)S(1)}, f32[1,128]{1,0:T(1,128)S(1)}, u32[]{:S(2)}, u32[]{:S(2)}) collective-permute-start(f32[1,128]{1,0:T(1,128)S(1)} %slice_maximum_fusion.2), channel_id=1, source_target_pairs={{0,24},{1,25},{2,26},{3,27},{4,28},{5,29},{6,30},{7,31},{8,16},{9,... | collective-permute-start | bytes 1544 | tf_op jit(solution)/shard_map/ppermute | solution.py:638
